TPU v7x, 128 devices: a whole 4x4x4 slice. The times are simulated.
128 devices in a mesh: fsdp: 8 (over z_hi, y), tp: 16 (over z_lo, x, core).
Axes of the slice: x: 4, y: 4, z: 4 (z_hi: 2, z_lo: 2; z = z_hi * 2 + z_lo), core: 2. Of those that a mesh axis runs over, the one named last changes fastest.
Arguments:
- tokens: bfloat16 [2048, 8192], P('fsdp', 'tp'), may hold values from -6 to 6
- out_grad: bfloat16 [2048, 8192], P('fsdp', 'tp'), may hold values from -6 to 6
- gate_weight: bfloat16 [8192, 2048], P('fsdp', 'tp'), may hold values from -0.0625 to 0.0625
- up_weight: bfloat16 [8192, 2048], P('fsdp', 'tp'), may hold values from -0.0625 to 0.0625
- down_weight: bfloat16 [2048, 8192], P('tp', 'fsdp'), may hold values from -0.125 to 0.125
Outputs:
- input_grad: bfloat16 [2048, 8192], P('fsdp', 'tp')
- gate_grad: float32 [8192, 2048], P('fsdp', 'tp')
- up_grad: float32 [8192, 2048], P('fsdp', 'tp')
- down_grad: float32 [2048, 8192], P('tp', 'fsdp')
All inputs are finite; a program needn't handle non-finite values.
Results may differ from a plain program's by a relative error of at most 0.0023.
Values may be sent and summed in bfloat16 or wider, within the bound.
A program may use at most 128 MiB of HBM per device.

v0:
```python
import math

import jax
import jax.numpy as jnp
from jax import lax
from jax.sharding import Mesh
from jax.sharding import PartitionSpec as P

FSDP = ("fsdp_0", "fsdp_1")


def laid_out(parts, dim):
    parts = jnp.moveaxis(parts, 0, dim)
    dims = parts.shape
    return parts.reshape(*dims[:dim], dims[dim] * dims[dim + 1], *dims[dim + 2 :])


def one_gather(arrays, axis, dims):
    line = jnp.concatenate([a.reshape(-1) for a in arrays])
    lines, at, outs = lax.all_gather(line, axis), 0, []
    for a, dim in zip(arrays, dims):
        parts = lines[:, at : at + a.size].reshape(-1, *a.shape)
        outs.append(laid_out(parts, dim))
        at += a.size
    return tuple(outs)


def stacked_from(value, axes, turns):
    parts = value[None]
    for k in turns:
        parts = lax.all_gather(parts, axes[k], axis=0, tiled=True)
    current = [lax.axis_size(axes[k]) for k in reversed(turns)]
    parts = parts.reshape(*current, *value.shape)
    turned = sorted(range(len(turns)), key=lambda place: turns[len(turns) - 1 - place])
    return parts.transpose(*turned, *range(len(turns), parts.ndim)).reshape(-1, *value.shape)


def gathered_by_axis(value, axes, turns, dim):
    return laid_out(stacked_from(value, axes, turns), dim)


def taken_in(value, axes, turns, dim, absorb, carry):
    everything = jax.tree.map(lambda part: gathered_by_axis(part, axes, turns, dim), value)
    return absorb(carry, everything, jnp.int32(0))


def own_rows(portion, rows, axis):
    count = rows * lax.axis_size(axis)
    return lax.psum_scatter(portion(jnp.int32(0), count), axis, scatter_dimension=0, tiled=True)


def column_term(left, right, start, count, factor):
    block = lax.dynamic_slice_in_dim(left, start, count, 1)
    product = lax.dot_general(
        block, right, (((0,), (0,)), ((), ())), preferred_element_type=jnp.float32
    )
    return product * factor


def shards(tokens, out_grad, gate_weight, up_weight, down_weight):
    factor = 1.0 / math.sqrt(tokens.shape[0] * lax.axis_size(FSDP))
    whole = lax.all_gather(tokens, "tp", axis=1, tiled=True)
    grads = lax.all_gather(out_grad, "tp", axis=1, tiled=True)
    gate_full, up_full = one_gather((gate_weight, up_weight), FSDP, (0, 0))
    gate = jnp.dot(whole, gate_full, preferred_element_type=jnp.float32)
    up = jnp.dot(whole, up_full, preferred_element_type=jnp.float32)

    def add_down(total, piece, start):
        columns = lax.dynamic_slice_in_dim(grads, start, piece.shape[1], 1)
        return total + lax.dot_general(
            columns, piece, (((1,), (1,)), ((), ())), preferred_element_type=jnp.float32
        )

    initial = jnp.zeros((whole.shape[0], down_weight.shape[0]), jnp.float32)
    hidden_grad = taken_in(down_weight, FSDP, (0, 1), 1, add_down, initial)
    squashed = jax.nn.sigmoid(gate)
    activated = gate * squashed
    slope = squashed * (1.0 + gate * (1.0 - squashed))
    hidden = (activated * up).astype(jnp.bfloat16)
    gate_delta = (hidden_grad * up * slope).astype(jnp.bfloat16)
    up_delta = (hidden_grad * activated).astype(jnp.bfloat16)

    def rows_term(start, count):
        gate_rows = lax.dynamic_slice_in_dim(gate_full, start, count, 0)
        up_rows = lax.dynamic_slice_in_dim(up_full, start, count, 0)
        first = lax.dot_general(
            gate_rows, gate_delta, (((1,), (1,)), ((), ())), preferred_element_type=jnp.float32
        )
        second = lax.dot_general(
            up_rows, up_delta, (((1,), (1,)), ((), ())), preferred_element_type=jnp.float32
        )
        return first + second

    local_rows = own_rows(rows_term, tokens.shape[1], "tp")
    input_grad = local_rows.T.astype(jnp.bfloat16)
    rows_here = gate_weight.shape[0]

    def joint_term(start, count):
        return jnp.concatenate(
            [
                column_term(whole, gate_delta, start, count, factor),
                column_term(whole, up_delta, start, count, factor),
                column_term(grads, hidden, start, count, factor),
            ],
            axis=1,
        )

    summed = own_rows(joint_term, rows_here, FSDP)
    width = gate_delta.shape[1]
    gate_grad = summed[:, :width]
    up_grad = summed[:, width : 2 * width]
    down_grad = summed[:, 2 * width :].T
    return (input_grad, gate_grad, up_grad, down_grad)


def solution(mesh):
    finer = Mesh(mesh.devices.reshape(2, 4, mesh.shape["tp"]), ("fsdp_0", "fsdp_1", "tp"))
    return jax.shard_map(
        shards,
        mesh=finer,
        in_specs=(P(FSDP, "tp"), P(FSDP, "tp"), P(FSDP, "tp"), P(FSDP, "tp"), P("tp", FSDP)),
        out_specs=(P(FSDP, "tp"), P(FSDP, "tp"), P(FSDP, "tp"), P("tp", FSDP)),
        check_vma=False,
    )
```

profile of v0, /device:TPU:8, one launch (start us, length us, event | category | flops | bytes accessed | tf_op | source)
XLA Modules:
  0.0 448.3 jit_solution(1478735136044264735)
XLA Ops:
  7.2 13.0 %all-gather.1 = bf16[256,1024]{1,0:T(8,128)(2,1)} all-gather(bf16[128,1024]{1,0:T(8,128)(2,1)} %param.9), channel_id=3, replica_groups=mesh['fsdp_0'=2,'fsdp_1'=4,'tp'=16] {'fsdp_0'}, dimensions={0}, use_global_device_ids=true | all-gather | bytes 786432 | tf_op jit(solution)/shard_map/all_gather | solution.py:31
  20.3 1.9 pad_maximum_fusion.1
  22.3 0.7 all-gather.11.cloned.1.call-update
  23.0 0.5 all-gather.7.cloned.1.call-update
  23.6 26.6 %all-gather.9.cloned.1.call-done = bf16[8,128,1024]{2,1,0:T(8,128)(2,1)} async-done(((bf16[2,128,1024]{2,1,0:T(8,128)(2,1)}), bf16[8,128,1024]{2,1,0:T(8,128)(2,1)}) %all-gather.9.cloned.1.call-update) | async-done | bytes 2097168 | tf_op jit(solution)/shard_map/all_gather | solution.py:31
  50.2 1.9 copy.27
  52.0 2.4 copy.28
  54.4 69.9 %all-gather.13.cloned.1.call-done = bf16[2097152]{0:T(1024)(128)(2,1)} async-done(((bf16[262144]{0:T(1024)(128)(2,1)}), bf16[2097152]{0:T(1024)(128)(2,1)}) %all-gather.13.cloned.1.call-update) | async-done | bytes 4194320 | tf_op jit(solution)/shard_map/all_gather | solution.py:20
  124.4 5.9 %reshape.28 = bf16[8,262144]{1,0:T(8,128)(2,1)} reshape(bf16[2097152]{0:T(1024)(128)(2,1)} %all-gather.13.cloned.1.call-done) | data formatting | bytes 8388608 | tf_op jit(solution)/shard_map/all_gather | solution.py:20
  130.2 3.9 fusion.6
  134.1 2.3 reshape_reshape.6
  136.4 2.5 reshape_reshape.7
  138.9 23.1 %all-gather.11.cloned.1.call-done = bf16[256,8192]{1,0:T(8,128)(2,1)} async-done(((bf16[256,512]{1,0:T(8,128)(2,1)}), bf16[256,8192]{1,0:T(8,128)(2,1)}) %all-gather.11.cloned.1.call-update) | async-done | bytes 4194320 | tf_op jit(solution)/shard_map/all_gather | solution.py:62
  162.1 4.2 convolution_bitcast_fusion
  166.3 1.3 convolution_bitcast_fusion.1
  167.7 33.2 %all-gather.7.cloned.1.call-done = bf16[256,8192]{1,0:T(8,128)(2,1)} async-done(((bf16[256,512]{1,0:T(8,128)(2,1)}), bf16[256,8192]{1,0:T(8,128)(2,1)}) %all-gather.7.cloned.1.call-update) | async-done | bytes 4194320 | tf_op jit(solution)/shard_map/all_gather | solution.py:63
  200.8 4.2 multiply_convert_fusion.1
  205.1 1.2 fusion.7
  206.4 4.5 %convolution_add_fusion = f32[8192,256]{1,0:T(8,128)} fusion(f32[8192,256]{1,0:T(8,128)S(1)} %fusion.7, bf16[8192,128]{1,0:T(8,128)(2,1)S(1)} %reshape_reshape.7, bf16[256,128]{1,0:T(8,128)(2,1)S(1)} %get-tuple-element.25), kind=kOutput, calls=%fused_computation.1 | convolution fusion | flops 538968064 | bytes 18939904 | tf_op jit(solution)/shard_map/dot_general | solution.py:89
  210.9 0.2 reduce-scatter.5.cloned.1.call-start
  211.1 3.3 fusion.1
  214.6 0.9 fusion.2
  215.5 1.3 copy-done.3
  216.7 1.0 fusion
  217.7 5.0 %pad_maximum_fusion = f32[8192,384]{0,1:T(8,128)} fusion(f32[8192,128]{0,1:T(8,128)S(1)} %fusion, f32[8192,128]{0,1:T(8,128)S(1)} %fusion.1, f32[8192,128]{0,1:T(8,128)S(1)} %fusion.2), kind=kLoop, calls=%fused_computation | loop fusion | flops 6291456 | bytes 25165824 | tf_op jit(solution)/shard_map/concatenate | solution.py:99
  222.7 63.2 %reduce-scatter.3.cloned.1.call-done = f32[512,256]{1,0:T(8,128)} async-done(((f32[8192,256]{1,0:T(8,128)}), f32[512,256]{1,0:T(8,128)}) %reduce-scatter.3.cloned.1.call-update) | async-done | bytes 524304 | tf_op jit(solution)/shard_map/reduce_scatter | solution.py:49
  285.9 1.1 convert_bitcast_fusion
  287.0 0.8 copy.31
  287.8 149.4 %reduce-scatter.5.cloned.1.call-done = f32[1024,384]{0,1:T(8,128)} async-done(((f32[8192,384]{0,1:T(8,128)}), f32[1024,384]{0,1:T(8,128)}) %reduce-scatter.5.cloned.1.call-update) | async-done | bytes 1572880 | tf_op jit(solution)/shard_map/reduce_scatter | solution.py:49
  437.2 2.3 slice_bitcast_fusion
  439.5 1.0 copy.32
  440.5 1.0 copy.33
  (16 shorter events, 0.5 us)
Async XLA Ops:
  7.2 43.0 %all-gather.9.cloned.1.call-start = ((), (), s32[]{:S(2)}) async-start(), calls=%async_computation.3 | async-start | bytes 2621440 | tf_op jit(solution)/shard_map/all_gather | solution.py:31
  20.3 104.1 %all-gather.13.cloned.1.call-start = ((), (), s32[]{:S(2)}) async-start(), calls=%async_computation.7 | async-start | bytes 4718592 | tf_op jit(solution)/shard_map/all_gather | solution.py:20
  22.2 139.8 %all-gather.11.cloned.1.call-start = ((), (), s32[]{:S(2)}) async-start(), calls=%async_computation.4 | async-start | bytes 4456448 | tf_op jit(solution)/shard_map/all_gather | solution.py:62
  22.9 177.9 %all-gather.7.cloned.1.call-start = ((), (), s32[]{:S(2)}) async-start(), calls=%async_computation.2 | async-start | bytes 4456448 | tf_op jit(solution)/shard_map/all_gather | solution.py:63
  23.5 262.4 %reduce-scatter.3.cloned.1.call-start = ((), (), s32[]{:S(2)}) async-start(), calls=%async_computation.5 | async-start | bytes 8912896 | tf_op jit(solution)/shard_map/reduce_scatter | solution.py:49
  162.0 4.3 copy-start
  200.8 4.3 copy-start.2
  210.9 226.3 %reduce-scatter.5.cloned.1.call-start = ((), (), s32[]{:S(2)}) async-start(), calls=%async_computation.6 | async-start | bytes 14155776 | tf_op jit(solution)/shard_map/reduce_scatter | solution.py:49
  211.1 3.5 copy-start.1
  214.6 2.2 copy-start.3
Sparse Core Ops, SparseCore 0:
  20.4 29.7 all-gather.8
  53.1 71.2 all-gather.12
  126.0 35.9 all-gather.10
  163.6 37.2 all-gather.6
  211.0 74.8 reduce-scatter.2
  289.7 147.4 reduce-scatter.4
where the time goes:
time: 450 us; the launch traced here: 448 us
  waiting for transfers between devices  367 us (82%)
  local copies, waits for them, and re-layouts  25.4 us (6%)
  matrix products  20.7 us (5%)
  between operations  14.2 us (3%)
  blocking collectives  13 us (3%)
  other arithmetic  7.91 us (2%)
    reduce_scatter x2, waiting for transfers between devices, own_rows(): lax.psum_scatter(portion(jnp.int32(0), count), axis, scatter_dimension=0,...  213 us
    all_gather x1, waiting for transfers between devices, one_gather(): lines, at, outs = (lax.all_gather(line, axis), 0, [])  69.9 us
    all_gather x1, waiting for transfers between devices, shards(): grads = lax.all_gather(out_grad, 'tp', axis=1, tiled=True)  33.2 us
    all_gather x1, waiting for transfers between devices, stacked_from(): parts = lax.all_gather(parts, axes[k], axis=0, tiled=True)  26.6 us
    all_gather x1, waiting for transfers between devices, shards(): whole = lax.all_gather(tokens, 'tp', axis=1, tiled=True)  23.1 us
    all_gather x1, blocking collectives, stacked_from(): parts = lax.all_gather(parts, axes[k], axis=0, tiled=True)  13 us
  transfers between devices with their start and end apart: 6, of which 6 were waited for; matrix products, arithmetic and copies ran while one was open for 9% of the time, Pallas kernels for 0%

commit v1 on v0

v1 whole, which is shorter than its diff:
```python
import functools
import math

import jax
import jax.numpy as jnp
from jax import lax
from jax.experimental import pallas as pl
from jax.experimental.pallas import tpu as pltpu
from jax.sharding import PartitionSpec as P

MESH = pl.DeviceIdType.MESH
F32, BF16 = jnp.float32, jnp.bfloat16
COPIES = 160


class Copy:
    def __init__(self, sems, src, dst, to, here=None):
        self.index = sems[2][0]
        sems[2][0] += 1
        send, recv = sems[0].at[self.index], sems[1].at[self.index]
        self.remote = pltpu.make_async_remote_copy(
            src_ref=src, dst_ref=dst, send_sem=send, recv_sem=recv, device_id=to, device_id_type=MESH
        )
        self.local = None if here is None else pltpu.make_async_copy(src, dst, recv)
        self.here = here

    def start(self):
        if self.here is None:
            self.remote.start()
        else:
            pl.when(self.here)(self.local.start)
            pl.when(jnp.logical_not(self.here))(self.remote.start)
        return self

    def wait(self):
        self.remote.wait_recv()

    def sent(self):
        if self.here is None:
            self.remote.wait_send()
        else:
            pl.when(jnp.logical_not(self.here))(self.remote.wait_send)


def nt(a, b):
    return lax.dot_general(a, b, (((1,), (1,)), ((), ())), preferred_element_type=F32)


def tn(a, b):
    return lax.dot_general(a, b, (((0,), (0,)), ((), ())), preferred_element_type=F32)


def nn(a, b):
    return jnp.dot(a, b, preferred_element_type=F32)


def kernel(
    factor,
    tok_ref, grd_ref, gate_ref, up_ref, down_ref,
    ig_ref, gg_ref, ug_ref, dg_ref,
    G, WG, WD, DS, DR, Q, RF, RN, DL, X, XF, XN, IB,
    Z, ZS, ZF, ZN, S, SX,
    SD, send, recv, local_sem,
):
    f, t = lax.axis_index("fsdp"), lax.axis_index("tp")
    h, y = lax.div(f, 4), lax.rem(f, 4)
    c = lax.rem(t, 2)
    x = lax.rem(lax.div(t, 2), 4)
    l = lax.div(t, 8)
    z = 2 * h + l
    sems = (send, recv, [0])
    sent = []

    def dev(x=x, y=y, z=z, c=c):
        return (lax.div(z, 2) * 4 + y, (lax.rem(z, 2) * 4 + x) * 2 + c)

    def copy(src, dst, to, here=None):
        made = Copy(sems, src, dst, to, here)
        sent.append(made)
        return made.start()

    def turn(v, k):
        return lax.rem(v + k + 4, 4)

    xp, xm, yp, ym, zp, zm = (turn(v, k) for v in (x, y, z) for k in (1, -1))
    yf, xf, zf = turn(y, 2), turn(x, 2), turn(z, 2)
    cc, ll = 1 - c, 1 - l
    zo = 2 * h + ll
    diagonal = x == y
    twin = dev(c=cc)

    barrier = pltpu.get_barrier_semaphore()
    peers = [
        twin, dev(x=xp), dev(x=xm), dev(y=yp), dev(y=ym),
        dev(z=zp), dev(z=zm), dev(z=zp, c=cc), dev(z=zm, c=cc), dev(x=y, y=x, z=zo),
    ]
    for peer in peers:
        pl.semaphore_signal(barrier, inc=1, device_id=peer, device_id_type=MESH)

    @pl.when(jnp.logical_not(diagonal))
    def _():
        pl.semaphore_signal(barrier, inc=1, device_id=dev(x=y, y=x), device_id_type=MESH)
        pl.semaphore_wait(barrier, len(peers) + 1)

    @pl.when(diagonal)
    def _():
        pl.semaphore_wait(barrier, len(peers))

    moved = {}
    arrays = (tok_ref, grd_ref)
    for a in range(2):
        for other in range(2):
            to_l = ll if other else l
            moved[a, other] = copy(
                arrays[a].at[pl.ds(pl.multiple_of(to_l * 128, 128), 128), :],
                G.at[a, l, y],
                dev(x=y, y=x, z=zo) if other else dev(x=y, y=x),
                None if other else diagonal,
            )

    def weight_piece(i, k):
        half = pl.multiple_of(k * 512, 512)
        if i < 2:
            return (gate_ref, up_ref)[i].at[pl.ds(half, 512), :]
        return down_ref.at[:, pl.ds(half, 512)]

    def weight_slot(i, at_z, core):
        at_h, block = lax.div(at_z, 2), lax.rem(at_z, 2) * 2 + core
        return WG.at[i, at_h, block] if i < 2 else WD.at[at_h, block]

    own_weights, from_twin, wp, wm = [], {}, {}, {}
    for i in range(3):
        mine = pltpu.make_async_copy(weight_piece(i, c), weight_slot(i, z, c), local_sem.at[i])
        mine.start()
        own_weights.append(mine)
        slot = weight_slot(i, z, c)
        wp[i, 0] = copy(weight_piece(i, c), slot, dev(z=zp))
        wm[i, 1] = copy(weight_piece(i, cc), slot, dev(z=zm, c=cc))
        wp[i, 1] = copy(weight_piece(i, cc), slot, dev(z=zp, c=cc))
        wm[i, 0] = copy(weight_piece(i, c), slot, dev(z=zm))
        from_twin[i] = copy(weight_piece(i, cc), slot, twin)

    far_w = {}

    def pass_weights(i):
        wp[i, 0].wait()
        slot = weight_slot(i, zm, c)
        far_w[i, 0] = copy(slot, slot, dev(z=zp))
        wm[i, 1].wait()
        slot = weight_slot(i, zp, cc)
        far_w[i, 1] = copy(slot, slot, dev(z=zm))

    def weights_here(i):
        own_weights[i].wait()
        from_twin[i].wait()
        wp[i, 1].wait()
        wm[i, 0].wait()
        far_w[i, 0].wait()
        far_w[i, 1].wait()

    gp, gm, far_g = {}, {}, {}
    for a in range(2):
        for other in range(2):
            moved[a, other].wait()
            slot = G.at[a, ll if other else l, x]
            gp[a, other] = copy(slot, slot, dev(x=xp))
            gm[a, other] = copy(slot, slot, dev(x=xm))

    def pass_tokens(a):
        gp[a, 0].wait()
        slot = G.at[a, l, xm]
        far_g[a, 0] = copy(slot, slot, dev(x=xp))
        gm[a, 1].wait()
        slot = G.at[a, ll, xp]
        far_g[a, 1] = copy(slot, slot, dev(x=xm))

    def tokens_here(a):
        gp[a, 1].wait()
        gm[a, 0].wait()
        far_g[a, 0].wait()
        far_g[a, 1].wait()

    pass_weights(0)
    pass_tokens(0)
    pass_weights(1)
    pass_tokens(1)
    pass_weights(2)

    def product(i, pair, l_to):
        total = None
        for k in range(2):
            rows = jnp.concatenate([G[min(i // 2, 1), k, pair * 2], G[min(i // 2, 1), k, pair * 2 + 1]], axis=0)
            if i < 2:
                right = jnp.concatenate([WG[i, k, 2 * l_to], WG[i, k, 2 * l_to + 1]], axis=1)
                term = nn(rows, right)
            else:
                right = jnp.concatenate([WD[k, 2 * l_to], WD[k, 2 * l_to + 1]], axis=0)
                term = nt(rows, right)
            total = term if total is None else total + term
        return total

    to_twin = {}

    def multiply(i):
        for l_to in range(2):
            DS[i, :, l_to] = product(i, cc, l_to).reshape(4, 64, 256)
        to_twin[i] = copy(DS.at[i], DR.at[i], twin)
        for l_to in range(2):
            Q[i, :, l_to] = product(i, c, l_to).reshape(4, 64, 256)

    yfar, ynear = {}, {}

    def sum_start(i):
        to_twin[i].wait()
        Q[i] += DR[i]
        yfar[i, 0] = copy(Q.at[i, yf, 0], RF.at[i, 0], dev(y=yp))
        yfar[i, 1] = copy(Q.at[i, yf, 1], RF.at[i, 1], dev(y=ym))
        ynear[i, 0, 1] = copy(Q.at[i, yp, 1], RN.at[i, 0, 1], dev(y=yp))
        ynear[i, 1, 0] = copy(Q.at[i, ym, 0], RN.at[i, 1, 0], dev(y=ym))

    def sum_middle(i):
        yfar[i, 0].wait()
        Q[i, yp, 0] += RF[i, 0]
        ynear[i, 0, 0] = copy(Q.at[i, yp, 0], RN.at[i, 0, 0], dev(y=yp))
        yfar[i, 1].wait()
        Q[i, ym, 1] += RF[i, 1]
        ynear[i, 1, 1] = copy(Q.at[i, ym, 1], RN.at[i, 1, 1], dev(y=ym))

    def sum_end(i, half):
        return Q[i, y, half] + RN[i, 0, half] + RN[i, 1, half]

    tokens_here(0)
    weights_here(0)
    multiply(0)
    sum_start(0)
    weights_here(1)
    multiply(1)
    sum_middle(0)
    sum_start(1)
    tokens_here(1)
    weights_here(2)
    multiply(2)
    sum_middle(1)
    sum_start(2)
    sum_middle(2)
    for i in range(3):
        for side in range(2):
            for half in range(2):
                ynear[i, side, half].wait()

    for half in range(2):
        gate, up, hidden_grad = sum_end(0, half), sum_end(1, half), sum_end(2, half)
        squashed = jax.nn.sigmoid(gate)
        activated = gate * squashed
        slope = squashed * (1.0 + gate * (1.0 - squashed))
        DL[c, y, 0, half] = (hidden_grad * up * slope).astype(BF16)
        DL[c, y, 1, half] = (hidden_grad * activated).astype(BF16)
        DL[c, y, 2, half] = (activated * up).astype(BF16)

    dp, dm, far_d, over = {}, {}, {}, []
    first, second = pl.ds(0, 32), pl.ds(32, 32)

    def delta_part(at_y, rows):
        return DL.at[c, at_y, :, :, rows]

    dp[0] = copy(delta_part(y, first), delta_part(y, first), dev(y=yp))
    dm[1] = copy(delta_part(y, second), delta_part(y, second), dev(y=ym))
    dp[1] = copy(delta_part(y, second), delta_part(y, second), dev(y=yp))
    dm[0] = copy(delta_part(y, first), delta_part(y, first), dev(y=ym))
    over.append(copy(DL.at[c, y], DL.at[c, y], twin))
    dp[0].wait()
    far_d[0] = copy(delta_part(ym, first), delta_part(ym, first), dev(y=yp))
    dm[1].wait()
    far_d[1] = copy(delta_part(yp, second), delta_part(yp, second), dev(y=ym))
    dp[1].wait()
    over.append(copy(DL.at[c, ym], DL.at[c, ym], twin))
    dm[0].wait()
    over.append(copy(DL.at[c, yp], DL.at[c, yp], twin))
    far_d[0].wait()
    far_d[1].wait()
    over.append(copy(DL.at[c, yf], DL.at[c, yf], twin))
    for made in over:
        made.wait()

    def delta(kind, l_to, core):
        return jnp.concatenate([DL[core, k, kind, l_to] for k in range(4)], axis=0)

    def delta_all(kind, l_to):
        return jnp.concatenate([delta(kind, l_to, 0), delta(kind, l_to, 1)], axis=0)

    def gathered(a, k):
        return G[a, k].reshape(512, 512)

    def grads_of_weights(i):
        for k in range(2):
            for m in range(2):
                if i < 2:
                    Z[i, 2 * k + m] = tn(gathered(0, k), delta_all(i, m)).reshape(2, 256, 256)
                else:
                    block = tn(delta_all(2, m), gathered(1, k))
                    for j in range(2):
                        Z[2, 2 * k + m, j] = jnp.concatenate(
                            [block[j * 128 : j * 128 + 128, :256], block[j * 128 : j * 128 + 128, 256:]], axis=0
                        )

    zfar, znear = {}, {}

    def wsum_start(i):
        ZS[i, 0] = Z[i, zf].astype(BF16)
        ZS[i, 1, 1] = Z[i, zp, 1].astype(BF16)
        ZS[i, 2, 0] = Z[i, zm, 0].astype(BF16)
        zfar[i, 0] = copy(ZS.at[i, 0, 0], ZF.at[i, 0], dev(z=zp))
        zfar[i, 1] = copy(ZS.at[i, 0, 1], ZF.at[i, 1], dev(z=zm))
        znear[i, 0, 1] = copy(ZS.at[i, 1, 1], ZN.at[i, 0, 1], dev(z=zp))
        znear[i, 1, 0] = copy(ZS.at[i, 2, 0], ZN.at[i, 1, 0], dev(z=zm))

    def wsum_middle(i):
        zfar[i, 0].wait()
        ZS[i, 1, 0] = (Z[i, zp, 0] + ZF[i, 0].astype(F32)).astype(BF16)
        znear[i, 0, 0] = copy(ZS.at[i, 1, 0], ZN.at[i, 0, 0], dev(z=zp))
        zfar[i, 1].wait()
        ZS[i, 2, 1] = (Z[i, zm, 1] + ZF[i, 1].astype(F32)).astype(BF16)
        znear[i, 1, 1] = copy(ZS.at[i, 2, 1], ZN.at[i, 1, 1], dev(z=zm))

    def wsum_end(i):
        for side in range(2):
            for half in range(2):
                znear[i, side, half].wait()
        return [
            (Z[i, z, half] + ZN[i, 0, half].astype(F32) + ZN[i, 1, half].astype(F32)) * factor
            for half in range(2)
        ]

    def input_term(pair, k):
        total = None
        for kind in range(2):
            left = jnp.concatenate([delta_pair(kind, pair, 0), delta_pair(kind, pair, 1)], axis=1)
            right = jnp.concatenate([WG[kind, k, b] for b in range(4)], axis=1)
            term = nt(left, right)
            total = term if total is None else total + term
        return total

    def delta_pair(kind, pair, l_to):
        return delta(kind, l_to, pair)

    xfar, xnear = {}, {}

    def isum_start():
        xfar[0] = copy(X.at[xf, 0], XF.at[0], dev(x=xp))
        xfar[1] = copy(X.at[xf, 1], XF.at[1], dev(x=xm))
        xnear[0, 1] = copy(X.at[xp, 1], XN.at[0, 1], dev(x=xp))
        xnear[1, 0] = copy(X.at[xm, 0], XN.at[1, 0], dev(x=xm))

    def isum_middle():
        xfar[0].wait()
        X[xp, 0] += XF[0]
        xnear[0, 0] = copy(X.at[xp, 0], XN.at[0, 0], dev(x=xp))
        xfar[1].wait()
        X[xm, 1] += XF[1]
        xnear[1, 1] = copy(X.at[xm, 1], XN.at[1, 1], dev(x=xm))

    grads_of_weights(0)
    wsum_start(0)
    for pair in range(2):
        for k in range(2):
            term = input_term(pair, k)
            X[2 * pair, k] = term[:128]
            X[2 * pair + 1, k] = term[128:]
    isum_start()
    grads_of_weights(1)
    wsum_start(1)
    grads_of_weights(2)
    wsum_start(2)
    wsum_middle(0)
    isum_middle()
    wsum_middle(1)
    wsum_middle(2)

    back = {}
    for side in range(2):
        for half in range(2):
            xnear[side, half].wait()
    for k in range(2):
        IB[k] = (X[x, k] + XN[0, k] + XN[1, k]).astype(BF16)
    for other in range(2):
        k = ll if other else l
        back[other] = copy(
            IB.at[k],
            ig_ref.at[pl.ds(pl.multiple_of(l * 128, 128), 128), :],
            dev(x=y, y=x, z=zo) if other else dev(x=y, y=x),
            None if other else diagonal,
        )

    last = []
    half_at = pl.multiple_of(c * 512, 512)
    for i in range(2):
        out = (gg_ref, ug_ref)[i]
        done = wsum_end(i)
        for half in range(2):
            low, high = done[half][:, :128], done[half][:, 128:]
            SX[i, pl.ds(half * 256, 256), :] = jnp.where(c == 0, high, low)
            S[i, pl.ds(half * 256, 256), :] = jnp.where(c == 0, low, high)
        rows = pl.ds(half_at, 512)
        last.append(copy(SX.at[i], out.at[rows, :], twin))
        out[rows, :] = S[i]
    done = wsum_end(2)
    blocks = [jnp.concatenate([part[:128], part[128:]], axis=1) for part in done]
    columns = pl.ds(half_at, 512)
    SD[...] = jnp.where(c == 0, blocks[1], blocks[0])
    last.append(copy(SD, dg_ref.at[:, columns], twin))
    dg_ref[:, columns] = jnp.where(c == 0, blocks[0], blocks[1])
    for made in [*last, *back.values()]:
        made.wait()
    for made in sent:
        made.sent()


def solution(mesh):
    def shards(tokens, out_grad, gate_weight, up_weight, down_weight):
        factor = 1.0 / math.sqrt(tokens.shape[0] * mesh.shape["fsdp"])
        vmem = pl.BlockSpec(memory_space=pltpu.VMEM)
        return pl.pallas_call(
            functools.partial(kernel, factor),
            out_shape=(
                jax.ShapeDtypeStruct((256, 512), BF16),
                jax.ShapeDtypeStruct((1024, 128), F32),
                jax.ShapeDtypeStruct((1024, 128), F32),
                jax.ShapeDtypeStruct((128, 1024), F32),
            ),
            in_specs=[vmem] * 5,
            out_specs=(vmem,) * 4,
            scratch_shapes=[
                pltpu.VMEM((2, 2, 4, 128, 512), BF16),
                pltpu.VMEM((2, 2, 4, 512, 128), BF16),
                pltpu.VMEM((2, 4, 128, 512), BF16),
                pltpu.VMEM((3, 4, 2, 64, 256), F32),
                pltpu.VMEM((3, 4, 2, 64, 256), F32),
                pltpu.VMEM((3, 4, 2, 64, 256), F32),
                pltpu.VMEM((3, 2, 64, 256), F32),
                pltpu.VMEM((3, 2, 2, 64, 256), F32),
                pltpu.VMEM((2, 4, 3, 2, 64, 256), BF16),
                pltpu.VMEM((4, 2, 128, 512), F32),
                pltpu.VMEM((2, 128, 512), F32),
                pltpu.VMEM((2, 2, 128, 512), F32),
                pltpu.VMEM((2, 128, 512), BF16),
                pltpu.VMEM((3, 4, 2, 256, 256), F32),
                pltpu.VMEM((3, 3, 2, 256, 256), BF16),
                pltpu.VMEM((3, 2, 256, 256), BF16),
                pltpu.VMEM((3, 2, 2, 256, 256), BF16),
                pltpu.VMEM((2, 512, 128), F32),
                pltpu.VMEM((2, 512, 128), F32),
                pltpu.VMEM((128, 512), F32),
                pltpu.SemaphoreType.DMA((COPIES,)),
                pltpu.SemaphoreType.DMA((COPIES,)),
                pltpu.SemaphoreType.DMA((3,)),
            ],
            compiler_params=pltpu.CompilerParams(
                collective_id=0, has_side_effects=True, vmem_limit_bytes=60 * 1024 * 1024
            ),
        )(tokens, out_grad, gate_weight, up_weight, down_weight)

    return jax.shard_map(
        shards,
        mesh=mesh,
        in_specs=(P("fsdp", "tp"),) * 4 + (P("tp", "fsdp"),),
        out_specs=(P("fsdp", "tp"),) * 3 + (P("tp", "fsdp"),),
        check_vma=False,
    )
```

time: 450 us -> 118 us (0.26)
  the two profiles are of different devices: /device:TPU:8 before, /device:TPU:39 now
where the time goes in v1:
time: 118 us
  Pallas kernels  113 us (96%)
  local copies, waits for them, and re-layouts  4.98 us (4%)
    pallas_call x1, Pallas kernels, shards(): pl.pallas_call(functools.partial(kernel, factor), out_shape=(jax.ShapeDty...  113 us
    unnamed x10, local copies, waits for them, and re-layouts  4.98 us

profile of v1, /device:TPU:39, one launch (start us, length us, event | category | flops | bytes accessed | tf_op | source)
XLA Modules:
  0.0 118.2 jit_solution(745994459594696660)
XLA Ops:
  0.6 112.6 %shard_map.84 = (bf16[256,512]{1,0:T(8,128)(2,1)}, f32[1024,128]{1,0:T(8,128)}, f32[1024,128]{1,0:T(8,128)}, f32[128,1024]{1,0:T(8,128)}) custom-call(bf16[256,512]{1,0:T(8,128)(2,1)} %tok_ref.1, bf16[256,512]{1,0:T(8,128)(2,1)} %grd_ref.1, bf16[1024,128]{1,0:T(8,128)(2,1)} %gate_ref.1, bf16[1024,128]{1,0:T(8,128)(2,1)} %up_ref.1, bf16[128,1024]{1,0:T(8,128)(2,1)} %down_ref.1), custom_call_target="tpu_custom_call" | custom-call | tf_op jit(solution)/shard_map/pallas_call | solution.py:422
  113.2 0.0 copy-start.2
  113.2 1.7 %copy.13 = bf16[256,512]{1,0:T(8,128)(2,1)} copy(bf16[256,512]{1,0:T(8,128)(2,1)} %get-tuple-element.8) | data formatting | bytes 524288
  114.9 0.0 copy-done.2
  114.9 0.0 copy-start.1
  114.9 0.8 copy.14
  115.7 0.4 copy-done.1
  116.2 0.0 copy-start
  116.2 0.8 copy.15
  117.0 0.4 copy-done
  117.4 0.8 copy.16
Async XLA Ops:
  113.2 1.7 %copy-start.2 = (f32[1024,128]{1,0:T(8,128)S(1)}, f32[1024,128]{1,0:T(8,128)}, u32[]{:S(2)}) copy-start(f32[1024,128]{1,0:T(8,128)} %get-tuple-element.9) | copy-start | bytes 1572868
  114.9 1.2 %copy-start.1 = (f32[1024,128]{1,0:T(8,128)S(1)}, f32[1024,128]{1,0:T(8,128)}, u32[]{:S(2)}) copy-start(f32[1024,128]{1,0:T(8,128)} %get-tuple-element.10) | copy-start | bytes 1572868
  116.2 1.2 %copy-start = (f32[128,1024]{1,0:T(8,128)S(1)}, f32[128,1024]{1,0:T(8,128)}, u32[]{:S(2)}) copy-start(f32[128,1024]{1,0:T(8,128)} %get-tuple-element.11) | copy-start | bytes 1572868

commit v2 on v1

--- a/solution.py
+++ b/solution.py
@@ -92,15 +92,20 @@
     barrier = pltpu.get_barrier_semaphore()
     peers = [
         twin, dev(x=xp), dev(x=xm), dev(y=yp), dev(y=ym),
-        dev(z=zp), dev(z=zm), dev(z=zp, c=cc), dev(z=zm, c=cc), dev(x=y, y=x, z=zo),
+        dev(z=zp), dev(z=zm), dev(z=zp, c=cc), dev(z=zm, c=cc),
     ]
+    for e in range(4):
+        there, back_there = dict(x=turn(y, e), y=x), dict(x=y, y=turn(x, -e))
+        peers += [dev(z=zo, **there), dev(z=zo, **back_there)]
+        if e > 0:
+            peers += [dev(**there), dev(**back_there)]
     for peer in peers:
         pl.semaphore_signal(barrier, inc=1, device_id=peer, device_id_type=MESH)
 
     @pl.when(jnp.logical_not(diagonal))
     def _():
-        pl.semaphore_signal(barrier, inc=1, device_id=dev(x=y, y=x), device_id_type=MESH)
-        pl.semaphore_wait(barrier, len(peers) + 1)
+        pl.semaphore_signal(barrier, inc=2, device_id=dev(x=y, y=x), device_id_type=MESH)
+        pl.semaphore_wait(barrier, len(peers) + 2)
 
     @pl.when(diagonal)
     def _():
@@ -111,12 +116,14 @@
     for a in range(2):
         for other in range(2):
             to_l = ll if other else l
-            moved[a, other] = copy(
-                arrays[a].at[pl.ds(pl.multiple_of(to_l * 128, 128), 128), :],
-                G.at[a, l, y],
-                dev(x=y, y=x, z=zo) if other else dev(x=y, y=x),
-                None if other else diagonal,
-            )
+            for e in range(4):
+                to_x = turn(y, e)
+                moved[a, other, e] = copy(
+                    arrays[a].at[pl.ds(pl.multiple_of(to_l * 128 + to_x * 32, 32), 32), :],
+                    G.at[a, l, to_x, pl.ds(pl.multiple_of(y * 32, 32), 32), :],
+                    dev(x=to_x, y=x, z=zo if other else z),
+                    diagonal if e == 0 and not other else None,
+                )
 
     def weight_piece(i, k):
         half = pl.multiple_of(k * 512, 512)
@@ -161,7 +168,8 @@
     gp, gm, far_g = {}, {}, {}
     for a in range(2):
         for other in range(2):
-            moved[a, other].wait()
+            for e in range(4):
+                moved[a, other, e].wait()
             slot = G.at[a, ll if other else l, x]
             gp[a, other] = copy(slot, slot, dev(x=xp))
             gm[a, other] = copy(slot, slot, dev(x=xm))
@@ -384,12 +392,14 @@
         IB[k] = (X[x, k] + XN[0, k] + XN[1, k]).astype(BF16)
     for other in range(2):
         k = ll if other else l
-        back[other] = copy(
-            IB.at[k],
-            ig_ref.at[pl.ds(pl.multiple_of(l * 128, 128), 128), :],
-            dev(x=y, y=x, z=zo) if other else dev(x=y, y=x),
-            None if other else diagonal,
-        )
+        for e in range(4):
+            to_y = turn(x, -e)
+            back[other, e] = copy(
+                IB.at[k, pl.ds(pl.multiple_of(to_y * 32, 32), 32), :],
+                ig_ref.at[pl.ds(pl.multiple_of(l * 128 + x * 32, 32), 32), :],
+                dev(x=y, y=to_y, z=zo if other else z),
+                diagonal if e == 0 and not other else None,
+            )
 
     last = []
     half_at = pl.multiple_of(c * 512, 512)

time: 118 us -> 110 us (0.932)
  the two profiles are of different devices: /device:TPU:39 before, /device:TPU:8 now
where the time goes in v2:
time: 110 us; the launch traced here: 109 us
  Pallas kernels  103 us (94%)
  local copies, waits for them, and re-layouts  4.98 us (5%)
    pallas_call x1, Pallas kernels, shards(): pl.pallas_call(functools.partial(kernel, factor), out_shape=(jax.ShapeDty...  103 us
    unnamed x10, local copies, waits for them, and re-layouts  4.98 us

profile of v2, /device:TPU:8, one launch (start us, length us, event | category | flops | bytes accessed | tf_op | source)
XLA Modules:
  0.0 108.9 jit_solution(8074893583423930788)
XLA Ops:
  0.6 103.2 %shard_map.84 = (bf16[256,512]{1,0:T(8,128)(2,1)}, f32[1024,128]{1,0:T(8,128)}, f32[1024,128]{1,0:T(8,128)}, f32[128,1024]{1,0:T(8,128)}) custom-call(bf16[256,512]{1,0:T(8,128)(2,1)} %tok_ref.1, bf16[256,512]{1,0:T(8,128)(2,1)} %grd_ref.1, bf16[1024,128]{1,0:T(8,128)(2,1)} %gate_ref.1, bf16[1024,128]{1,0:T(8,128)(2,1)} %up_ref.1, bf16[128,1024]{1,0:T(8,128)(2,1)} %down_ref.1), custom_call_target="tpu_custom_call" | custom-call | tf_op jit(solution)/shard_map/pallas_call | solution.py:432
  103.9 0.0 copy-start.2
  103.9 1.7 %copy.13 = bf16[256,512]{1,0:T(8,128)(2,1)} copy(bf16[256,512]{1,0:T(8,128)(2,1)} %get-tuple-element.8) | data formatting | bytes 524288
  105.6 0.0 copy-done.2
  105.6 0.0 copy-start.1
  105.6 0.8 copy.14
  106.4 0.4 copy-done.1
  106.8 0.0 copy-start
  106.8 0.8 copy.15
  107.6 0.4 copy-done
  108.1 0.8 copy.16
Async XLA Ops:
  103.9 1.7 %copy-start.2 = (f32[1024,128]{1,0:T(8,128)S(1)}, f32[1024,128]{1,0:T(8,128)}, u32[]{:S(2)}) copy-start(f32[1024,128]{1,0:T(8,128)} %get-tuple-element.9) | copy-start | bytes 1572868
  105.6 1.2 %copy-start.1 = (f32[1024,128]{1,0:T(8,128)S(1)}, f32[1024,128]{1,0:T(8,128)}, u32[]{:S(2)}) copy-start(f32[1024,128]{1,0:T(8,128)} %get-tuple-element.10) | copy-start | bytes 1572868
  106.8 1.2 %copy-start = (f32[128,1024]{1,0:T(8,128)S(1)}, f32[128,1024]{1,0:T(8,128)}, u32[]{:S(2)}) copy-start(f32[128,1024]{1,0:T(8,128)} %get-tuple-element.11) | copy-start | bytes 1572868

commit v3 on v0

v3 whole, which is shorter than its diff:
```python
import functools
import math

import jax
import jax.numpy as jnp
from jax import lax
from jax.experimental import pallas as pl
from jax.experimental.pallas import tpu as pltpu
from jax.sharding import PartitionSpec as P

MESH = pl.DeviceIdType.MESH
F32, BF16 = jnp.float32, jnp.bfloat16
COPIES = 200


class Copy:
    def __init__(self, sems, src, dst, to, here=None):
        index = sems[2][0]
        sems[2][0] += 1
        send, recv = sems[0].at[index], sems[1].at[index]
        self.remote = pltpu.make_async_remote_copy(
            src_ref=src, dst_ref=dst, send_sem=send, recv_sem=recv, device_id=to, device_id_type=MESH
        )
        self.local = None if here is None else pltpu.make_async_copy(src, dst, recv)
        self.here = here
        self.done = False

    def start(self):
        if self.here is None:
            self.remote.start()
        else:
            pl.when(self.here)(self.local.start)
            pl.when(jnp.logical_not(self.here))(self.remote.start)
        return self

    def wait(self):
        if not self.done:
            self.remote.wait_recv()
        self.done = True

    def sent(self):
        if self.here is None:
            self.remote.wait_send()
        else:
            pl.when(jnp.logical_not(self.here))(self.remote.wait_send)


def nt(a, b):
    return lax.dot_general(a, b, (((1,), (1,)), ((), ())), preferred_element_type=F32)


def tn(a, b):
    return lax.dot_general(a, b, (((0,), (0,)), ((), ())), preferred_element_type=F32)


def nn(a, b):
    return jnp.dot(a, b, preferred_element_type=F32)


def kernel(
    factor,
    tok_ref, grd_ref, gate_ref, up_ref, down_ref,
    ig_ref, gg_ref, ug_ref, dg_ref,
    TV, WV, WDV, G, GT, WG, WD, PS, DR, RF, RN, GU, DL, X, XF, XN, IB,
    Z, ZS, ZF, ZN, S, SX, SD,
    send, recv, local_sem, load_sem,
):
    f, t = lax.axis_index("fsdp"), lax.axis_index("tp")
    h, y = lax.div(f, 4), lax.rem(f, 4)
    c = lax.rem(t, 2)
    x = lax.rem(lax.div(t, 2), 4)
    l = lax.div(t, 8)
    z = 2 * h + l
    sems = (send, recv, [0])
    sent = []

    def dev(x=x, y=y, z=z, c=c):
        return (lax.div(z, 2) * 4 + y, (lax.rem(z, 2) * 4 + x) * 2 + c)

    def copy(src, dst, to, here=None):
        made = Copy(sems, src, dst, to, here)
        sent.append(made)
        return made.start()

    def turn(v, k):
        return lax.rem(v + k + 4, 4)

    xp, xm, yp, ym, zp, zm = (turn(v, k) for v in (x, y, z) for k in (1, -1))
    yf, xf, zf = turn(y, 2), turn(x, 2), turn(z, 2)
    cc, ll = 1 - c, 1 - l
    zo = 2 * h + ll
    zn = turn(z, 2 * l - 1)
    diagonal = x == y
    twin = dev(c=cc)

    loads = [
        pltpu.make_async_copy(src, dst, load_sem.at[n])
        for n, (src, dst) in enumerate(
            [(tok_ref, TV.at[0]), (grd_ref, TV.at[1]), (gate_ref, WV.at[0]), (up_ref, WV.at[1]), (down_ref, WDV)]
        )
    ]
    for load in loads:
        load.start()

    barrier = pltpu.get_barrier_semaphore()
    peers = [
        twin, dev(x=xp), dev(x=xm), dev(y=yp), dev(y=ym),
        dev(z=zp), dev(z=zm), dev(z=zp, c=cc), dev(z=zm, c=cc),
    ]
    for e in range(4):
        there, back_there = dict(x=turn(y, e), y=x), dict(x=y, y=turn(x, -e))
        peers += [dev(z=zo, **there), dev(z=zo, **back_there)]
        if e > 0:
            peers += [dev(**there), dev(**back_there)]
    for peer in peers:
        pl.semaphore_signal(barrier, inc=1, device_id=peer, device_id_type=MESH)

    @pl.when(jnp.logical_not(diagonal))
    def _():
        pl.semaphore_signal(barrier, inc=2, device_id=dev(x=y, y=x), device_id_type=MESH)
        pl.semaphore_wait(barrier, len(peers) + 2)

    @pl.when(diagonal)
    def _():
        pl.semaphore_wait(barrier, len(peers))

    moved = {}

    def move(a):
        loads[a].wait()
        for other in (1, 0):
            to_l = ll if other else l
            for e in range(4):
                to_x = turn(y, e)
                moved[a, other, e] = copy(
                    TV.at[a, pl.ds(pl.multiple_of(to_l * 128 + to_x * 32, 32), 32), :],
                    G.at[a, l, e // 2, to_x, pl.ds(e % 2 * 32, 32), :],
                    dev(x=to_x, y=x, z=zo if other else z),
                    diagonal if e == 0 and not other else None,
                )

    def weight_piece(i, k):
        half = pl.multiple_of(k * 512, 512)
        if i < 2:
            return WV.at[i, pl.ds(half, 512), :]
        return WDV.at[:, pl.ds(half, 512)]

    def weight_slot(i, at_z, core):
        at_h, block = lax.div(at_z, 2), lax.rem(at_z, 2) * 2 + core
        return WG.at[i, at_h, block] if i < 2 else WD.at[at_h, block]

    own_weights, from_twin, wn, wo, far_w = {}, {}, {}, {}, {}
    cores = (c, cc)

    def send_weights(i):
        loads[2 + i].wait()
        slot = weight_slot(i, z, c)
        mine = pltpu.make_async_copy(weight_piece(i, c), slot, local_sem.at[i])
        mine.start()
        own_weights[i] = mine
        from_twin[i] = copy(weight_piece(i, cc), slot, twin)

    def send_weights_to(i, s, over_n):
        to_z, made = (zn, wn) if over_n else (zo, wo)
        made[i, s] = copy(weight_piece(i, cores[s]), weight_slot(i, z, c), dev(z=to_z, c=cores[s]))

    def pass_weights(i, s):
        over_n = s == 0 or i == 0
        arrived, at_z, to_z = (wo, zo, zn) if over_n else (wn, zn, zo)
        arrived[i, s].wait()
        slot = weight_slot(i, at_z, cores[s])
        far_w[i, s] = copy(slot, slot, dev(z=to_z))

    def weights_here(i, part):
        if part == 0:
            for s in range(2):
                wn[i, s].wait()
                wo[i, s].wait()
        else:
            own_weights[i].wait()
            from_twin[i].wait()
            far_w[i, 0].wait()
            far_w[i, 1].wait()

    gp, gm, far_g = {}, {}, {}

    def spread(a, other):
        for e in range(4):
            moved[a, other, e].wait()
        slot = G.at[a, ll if other else l, :, x]
        gp[a, other] = copy(slot, slot, dev(x=xp))
        gm[a, other] = copy(slot, slot, dev(x=xm))

    def pass_tokens(a):
        gp[a, 0].wait()
        slot = G.at[a, l, :, xm]
        far_g[a, 0] = copy(slot, slot, dev(x=xp))
        gm[a, 1].wait()
        slot = G.at[a, ll, :, xp]
        far_g[a, 1] = copy(slot, slot, dev(x=xm))

    def tokens_here(a):
        gp[a, 1].wait()
        gm[a, 0].wait()
        far_g[a, 0].wait()
        far_g[a, 1].wait()

    sides = (ll, l)

    def gathered(a, k):
        return G[a, k].reshape(512, 512)

    def multiply(unit):
        parts, arrays_of, chunks = unit
        for part in range(*parts):
            l_to = sides[part]
            for i in range(*arrays_of):
                a = min(i // 2, 1)
                total = None
                for k in range(2):
                    rows = gathered(a, k) if chunks == (0, 2) else G[a, k, chunks[0]].reshape(256, 512)
                    if i < 2:
                        right = jnp.concatenate([WG[i, k, 2 * l_to], WG[i, k, 2 * l_to + 1]], axis=1)
                        term = nn(rows, right)
                    else:
                        right = jnp.concatenate([WD[k, 2 * l_to], WD[k, 2 * l_to + 1]], axis=0)
                        term = nt(rows, right)
                    total = term if total is None else total + term
                for half in range(2):
                    block = total[:, half * 128 : half * 128 + 128]
                    PS[part, i, chunks[0] : chunks[1], :, :, half] = block.reshape(
                        chunks[1] - chunks[0], 2, 4, 32, 128
                    )
        to_twin[unit] = copy(at(PS, unit, cc), at(DR, unit), twin)

    to_twin, yfar, ynear = {}, {}, {}

    def at(ref, unit, *more):
        return ref.at[(*(pl.ds(first, end - first) for first, end in unit), *more)]

    def over_unit(unit):
        parts, arrays_of, chunks = unit
        return [(p, i, q) for p in range(*parts) for i in range(*arrays_of) for q in range(*chunks)]

    def sum_start(unit):
        to_twin[unit].wait()
        for u in over_unit(unit):
            PS[(*u, c)] += DR[u]
        yfar[unit, 0] = copy(at(PS, unit, c, yf, 0), at(RF, unit, 0), dev(y=yp))
        yfar[unit, 1] = copy(at(PS, unit, c, yf, 1), at(RF, unit, 1), dev(y=ym))
        ynear[unit, 0, 1] = copy(at(PS, unit, c, yp, 1), at(RN, unit, 0, 1), dev(y=yp))
        ynear[unit, 1, 0] = copy(at(PS, unit, c, ym, 0), at(RN, unit, 1, 0), dev(y=ym))

    def sum_middle(unit):
        yfar[unit, 0].wait()
        for u in over_unit(unit):
            PS[(*u, c, yp, 0)] += RF[(*u, 0)]
        ynear[unit, 0, 0] = copy(at(PS, unit, c, yp, 0), at(RN, unit, 0, 0), dev(y=yp))
        yfar[unit, 1].wait()
        for u in over_unit(unit):
            PS[(*u, c, ym, 1)] += RF[(*u, 1)]
        ynear[unit, 1, 1] = copy(at(PS, unit, c, ym, 1), at(RN, unit, 1, 1), dev(y=ym))

    def sum_arrived(unit):
        for side in range(2):
            for half in range(2):
                ynear[unit, side, half].wait()

    def sum_end(part, i, q):
        return PS[part, i, q, c, y] + RN[part, i, q, 0] + RN[part, i, q, 1]

    def make_hidden(unit):
        sum_arrived(unit)
        for part in range(*unit[0]):
            for q in range(2):
                gate, up = sum_end(part, 0, q), sum_end(part, 1, q)
                GU[part, 0, q] = gate
                GU[part, 1, q] = up
                DL[part, c, y, 2, q] = (gate * jax.nn.sigmoid(gate) * up).astype(BF16)

    def make_deltas(unit):
        sum_arrived(unit)
        for part, _, q in over_unit(unit):
            gate, up, hidden_grad = GU[part, 0, q], GU[part, 1, q], sum_end(part, 2, q)
            squashed = jax.nn.sigmoid(gate)
            activated = gate * squashed
            slope = squashed * (1.0 + gate * (1.0 - squashed))
            DL[part, c, y, 0, q] = (hidden_grad * up * slope).astype(BF16)
            DL[part, c, y, 1, q] = (hidden_grad * activated).astype(BF16)

    dp, dm, far_d, over = {}, {}, {}, {}

    def delta_at(group, at_y, *half):
        parts, kinds, chunks = (pl.ds(first, end - first) for first, end in group)
        return DL.at[(parts, c, at_y, kinds, chunks, *half)]

    def give(group):
        for half in range(2):
            part = delta_at(group, y, half)
            dp[group, half] = copy(part, part, dev(y=yp))
            part = delta_at(group, y, 1 - half)
            dm[group, 1 - half] = copy(part, part, dev(y=ym))
        over[group] = [copy(delta_at(group, y), delta_at(group, y), twin)]

    def give_on(group):
        dp[group, 0].wait()
        part = delta_at(group, ym, 0)
        far_d[group, 0] = copy(part, part, dev(y=yp))
        dm[group, 1].wait()
        part = delta_at(group, yp, 1)
        far_d[group, 1] = copy(part, part, dev(y=ym))
        dp[group, 1].wait()
        over[group].append(copy(delta_at(group, ym), delta_at(group, ym), twin))
        dm[group, 0].wait()
        over[group].append(copy(delta_at(group, yp), delta_at(group, yp), twin))

    def give_end(group):
        far_d[group, 0].wait()
        far_d[group, 1].wait()
        over[group].append(copy(delta_at(group, yf), delta_at(group, yf), twin))

    def given(group):
        for made in over[group]:
            made.wait()

    def delta(kind, part, q):
        return jnp.concatenate([DL[part, :, :, kind, q, half].reshape(256, 128) for half in range(2)], axis=1)

    def delta_all(kind, part):
        return jnp.concatenate([delta(kind, part, 0), delta(kind, part, 1)], axis=0)

    halves = (h, 1 - h)

    def grads_of_weights(i, part):
        for r in range(2):
            if i < 2:
                Z[i, 2 * part + r] = nn(GT[halves[r]], delta_all(i, part)).reshape(2, 256, 256)
            else:
                block = tn(delta_all(2, part), gathered(1, halves[r]))
                for j in range(2):
                    Z[2, 2 * part + r, j] = jnp.concatenate(
                        [block[j * 128 : j * 128 + 128, :256], block[j * 128 : j * 128 + 128, 256:]], axis=0
                    )

    zfar, znear = {}, {}

    def wsum_near(i):
        ZS[i, 0, 1] = Z[i, 0, 1].astype(BF16)
        znear[i, 0, 1] = copy(ZS.at[i, 0, 1], ZN.at[i, 0, 1], dev(z=zo))
        ZS[i, 1, 0] = Z[i, 1, 0].astype(BF16)
        znear[i, 1, 0] = copy(ZS.at[i, 1, 0], ZN.at[i, 1, 0], dev(z=zn))

    def wsum_far(i):
        ZS[i, 2] = Z[i, 3].astype(BF16)
        zfar[i, 0] = copy(ZS.at[i, 2, 0], ZF.at[i, 0], dev(z=zn))
        zfar[i, 1] = copy(ZS.at[i, 2, 1], ZF.at[i, 1], dev(z=zo))

    def wsum_middle(i):
        zfar[i, 0].wait()
        ZS[i, 0, 0] = (Z[i, 0, 0] + ZF[i, 0].astype(F32)).astype(BF16)
        znear[i, 0, 0] = copy(ZS.at[i, 0, 0], ZN.at[i, 0, 0], dev(z=zo))
        zfar[i, 1].wait()
        ZS[i, 1, 1] = (Z[i, 1, 1] + ZF[i, 1].astype(F32)).astype(BF16)
        znear[i, 1, 1] = copy(ZS.at[i, 1, 1], ZN.at[i, 1, 1], dev(z=zn))

    last = []
    half_at = pl.ds(pl.multiple_of(c * 512, 512), 512)

    def wsum_end(i):
        for side in range(2):
            for half in range(2):
                znear[i, side, half].wait()
        done = [
            (Z[i, 2, half] + ZN[i, 0, half].astype(F32) + ZN[i, 1, half].astype(F32)) * factor
            for half in range(2)
        ]
        if i < 2:
            out = (gg_ref, ug_ref)[i]
            for half in range(2):
                low, high = done[half][:, :128], done[half][:, 128:]
                SX[i, pl.ds(half * 256, 256), :] = jnp.where(c == 0, high, low)
                S[i, pl.ds(half * 256, 256), :] = jnp.where(c == 0, low, high)
            last.append(copy(SX.at[i], out.at[half_at, :], twin))
            out[half_at, :] = S[i]
        else:
            blocks = [jnp.concatenate([part[:128], part[128:]], axis=1) for part in done]
            SD[...] = jnp.where(c == 0, blocks[1], blocks[0])
            last.append(copy(SD, dg_ref.at[:, half_at], twin))
            dg_ref[:, half_at] = jnp.where(c == 0, blocks[0], blocks[1])

    def input_rows(q):
        left = jnp.concatenate([delta(kind, part, q) for part in range(2) for kind in range(2)], axis=1)
        for k in range(2):
            right = jnp.concatenate(
                [WG[kind, k, 2 * sides[part] + b] for part in range(2) for kind in range(2) for b in range(2)], axis=1
            )
            X[q, :, k] = nt(left, right).reshape(4, 64, 512)

    xfar, xnear = {}, {}

    def isum_start(q):
        xfar[q, 0] = copy(X.at[q, xf, 0], XF.at[q, 0], dev(x=xp))
        xfar[q, 1] = copy(X.at[q, xf, 1], XF.at[q, 1], dev(x=xm))
        xnear[q, 0, 1] = copy(X.at[q, xp, 1], XN.at[q, 0, 1], dev(x=xp))
        xnear[q, 1, 0] = copy(X.at[q, xm, 0], XN.at[q, 1, 0], dev(x=xm))

    def isum_middle(q):
        xfar[q, 0].wait()
        X[q, xp, 0] += XF[q, 0]
        xnear[q, 0, 0] = copy(X.at[q, xp, 0], XN.at[q, 0, 0], dev(x=xp))
        xfar[q, 1].wait()
        X[q, xm, 1] += XF[q, 1]
        xnear[q, 1, 1] = copy(X.at[q, xm, 1], XN.at[q, 1, 1], dev(x=xm))

    def isum_end(q):
        for side in range(2):
            for half in range(2):
                xnear[q, side, half].wait()
        for k in range(2):
            IB[k, pl.ds(2 * q, 2)] = (X[q, x, k] + XN[q, 0, k] + XN[q, 1, k]).astype(BF16).reshape(2, 32, 512)

    back = {}

    def send_back(q):
        for other in (1, 0):
            for e in (2 * q, 2 * q + 1):
                back[other, e] = copy(
                    IB.at[ll if other else l, e],
                    ig_ref.at[pl.ds(pl.multiple_of(l * 128 + x * 32, 32), 32), :],
                    dev(x=y, y=turn(x, -e), z=zo if other else z),
                    diagonal if e == 0 and not other else None,
                )

    GATE_UP, HIDDEN = 0, 1
    both = (0, 2)
    gate_up = [((part, part + 1), both, both) for part in range(2)]
    down = [(both, (2, 3), (q, q + 1)) for q in range(2)]
    hidden = (both, (2, 3), both)
    deltas = [(both, both, (q, q + 1)) for q in range(2)]
    move(0)
    for i in range(3):
        send_weights(i)
        for s in range(2):
            send_weights_to(i, s, False)
            send_weights_to(i, s, True)
        if i == 0:
            move(1)
    spread(0, 0)
    spread(0, 1)
    spread(1, 0)
    pass_weights(0, 0)
    pass_tokens(0)
    spread(1, 1)
    pass_weights(0, 1)
    pass_weights(1, 1)
    pass_weights(1, 0)
    tokens_here(0)
    weights_here(0, 0)
    weights_here(1, 0)
    multiply(gate_up[0])
    pass_tokens(1)
    sum_start(gate_up[0])
    weights_here(0, 1)
    weights_here(1, 1)
    multiply(gate_up[1])
    pass_weights(2, 0)
    pass_weights(2, 1)
    sum_middle(gate_up[0])
    sum_start(gate_up[1])
    for k in range(2):
        GT[k] = gathered(0, k).T
    tokens_here(1)
    weights_here(2, 0)
    weights_here(2, 1)
    multiply(down[0])
    multiply(down[1])
    sum_middle(gate_up[1])
    make_hidden(gate_up[0])
    sum_start(down[0])
    sum_start(down[1])
    make_hidden(gate_up[1])
    give(hidden)
    sum_middle(down[0])
    sum_middle(down[1])
    give_on(hidden)
    make_deltas(down[0])
    give(deltas[0])
    make_deltas(down[1])
    give(deltas[1])
    give_end(hidden)
    given(hidden)
    grads_of_weights(2, 1)
    wsum_far(2)
    grads_of_weights(2, 0)
    wsum_near(2)
    give_on(deltas[0])
    give_on(deltas[1])
    give_end(deltas[0])
    give_end(deltas[1])
    given(deltas[0])
    input_rows(0)
    isum_start(0)
    wsum_middle(2)
    given(deltas[1])
    grads_of_weights(0, 1)
    wsum_far(0)
    grads_of_weights(0, 0)
    wsum_near(0)
    input_rows(1)
    isum_start(1)
    grads_of_weights(1, 1)
    wsum_far(1)
    grads_of_weights(1, 0)
    wsum_near(1)
    isum_middle(0)
    isum_middle(1)
    wsum_middle(0)
    wsum_middle(1)
    wsum_end(2)
    isum_end(0)
    send_back(0)
    isum_end(1)
    send_back(1)
    wsum_end(0)
    wsum_end(1)
    for made in [*last, *back.values()]:
        made.wait()
    for made in sent:
        assert made.done
        made.sent()


def put_out(a, b, c, d, a_out, b_out, c_out, d_out, sems):
    copies = [
        pltpu.make_async_copy(src, dst, sems.at[n])
        for n, (src, dst) in enumerate([(a, a_out), (b, b_out), (c, c_out), (d, d_out)])
    ]
    for made in copies:
        made.start()
    for made in copies:
        made.wait()


def solution(mesh):
    def shards(tokens, out_grad, gate_weight, up_weight, down_weight):
        factor = 1.0 / math.sqrt(tokens.shape[0] * mesh.shape["fsdp"])
        vmem = pl.BlockSpec(memory_space=pltpu.VMEM)
        made = pl.pallas_call(
            functools.partial(kernel, factor),
            out_shape=(
                pltpu.VMEM((256, 512), BF16),
                pltpu.VMEM((1024, 128), F32),
                pltpu.VMEM((1024, 128), F32),
                pltpu.VMEM((128, 1024), F32),
            ),
            in_specs=[pl.BlockSpec(memory_space=pl.ANY)] * 5,
            out_specs=(vmem,) * 4,
            scratch_shapes=[
                pltpu.VMEM((2, 256, 512), BF16),
                pltpu.VMEM((2, 1024, 128), BF16),
                pltpu.VMEM((128, 1024), BF16),
                pltpu.VMEM((2, 2, 2, 4, 64, 512), BF16),
                pltpu.VMEM((2, 512, 512), BF16),
                pltpu.VMEM((2, 2, 4, 512, 128), BF16),
                pltpu.VMEM((2, 4, 128, 512), BF16),
                pltpu.VMEM((2, 3, 2, 2, 4, 2, 32, 128), F32),
                pltpu.VMEM((2, 3, 2, 4, 2, 32, 128), F32),
                pltpu.VMEM((2, 3, 2, 2, 32, 128), F32),
                pltpu.VMEM((2, 3, 2, 2, 2, 32, 128), F32),
                pltpu.VMEM((2, 2, 2, 2, 32, 128), F32),
                pltpu.VMEM((2, 2, 4, 3, 2, 2, 32, 128), BF16),
                pltpu.VMEM((2, 4, 2, 64, 512), F32),
                pltpu.VMEM((2, 2, 64, 512), F32),
                pltpu.VMEM((2, 2, 2, 64, 512), F32),
                pltpu.VMEM((2, 4, 32, 512), BF16),
                pltpu.VMEM((3, 4, 2, 256, 256), F32),
                pltpu.VMEM((3, 3, 2, 256, 256), BF16),
                pltpu.VMEM((3, 2, 256, 256), BF16),
                pltpu.VMEM((3, 2, 2, 256, 256), BF16),
                pltpu.VMEM((2, 512, 128), F32),
                pltpu.VMEM((2, 512, 128), F32),
                pltpu.VMEM((128, 512), F32),
                pltpu.SemaphoreType.DMA((COPIES,)),
                pltpu.SemaphoreType.DMA((COPIES,)),
                pltpu.SemaphoreType.DMA((3,)),
                pltpu.SemaphoreType.DMA((5,)),
            ],
            compiler_params=pltpu.CompilerParams(
                collective_id=0, has_side_effects=True, vmem_limit_bytes=60 * 1024 * 1024
            ),
        )(tokens, out_grad, gate_weight, up_weight, down_weight)
        return pl.pallas_call(
            put_out,
            out_shape=tuple(jax.ShapeDtypeStruct(part.shape, part.dtype) for part in made),
            in_specs=[vmem] * 4,
            out_specs=(pl.BlockSpec(memory_space=pl.ANY),) * 4,
            scratch_shapes=[pltpu.SemaphoreType.DMA((4,))],
        )(*(pltpu.with_memory_space_constraint(part, pltpu.VMEM) for part in made))

    return jax.shard_map(
        shards,
        mesh=mesh,
        in_specs=(P("fsdp", "tp"),) * 4 + (P("tp", "fsdp"),),
        out_specs=(P("fsdp", "tp"),) * 3 + (P("tp", "fsdp"),),
        check_vma=False,
    )
```

time: 450 us -> 95.9 us (0.21)
  waiting for transfers between devices: 367 us -> 0 us
  Pallas kernels: 0 us -> 94.5 us
  local copies, waits for them, and re-layouts: 25.4 us -> 0 us
  matrix products: 20.7 us -> 0 us
  between operations: 14.2 us -> 0.64 us
  blocking collectives: 13 us -> 0 us
  other arithmetic: 7.91 us -> 0 us
    reduce_scatter x2 -> x0, waiting for transfers between devices: 213 us -> none  [own_rows(): lax.psum_scatter(portion(jnp.int32(0), count), axis, scatter_dimension=0,...]
    all_gather x4 -> x0, waiting for transfers between devices: 153 us -> none  [the longest x1 69.9 us: one_gather(): lines, at, outs = (lax.all_gather(line, axis), 0, [])]
    pallas_call x0 -> x2, Pallas kernels: none -> 94.5 us  [the longest x1 93.2 us: shards(): pl.pallas_call(functools.partial(kernel, factor), out_shape=(pltpu.VMEM((...]
    dot_general x8 -> x0, matrix products: 20.7 us -> none  [the longest x3 5.14 us: column_term(): lax.dot_general(block, right, (((0,), (0,)), ((), ())), preferred_element...]
    all_gather x1 -> x0, blocking collectives: 13 us -> none  [stacked_from(): parts = lax.all_gather(parts, axes[k], axis=0, tiled=True)]
    concatenate x2 -> x0, other arithmetic: 6.84 us -> none  [the longest x1 4.98 us: joint_term(): jnp.concatenate([column_term(whole, gate_delta, start, count, factor), co...]
    transpose x3 -> x0, local copies, waits for them, and re-layouts: 6.55 us -> none  [the longest x1 2.41 us: laid_out(): parts = jnp.moveaxis(parts, 0, dim)]
    all_gather x1 -> x0, local copies, waits for them, and re-layouts: 5.86 us -> none  [one_gather(): lines, at, outs = (lax.all_gather(line, axis), 0, [])]
  transfers between devices with their start and end apart: 6 -> 0, of which waited for: 6 -> 0; matrix products, arithmetic and copies ran while one was open for 9% -> 0% of each run, Pallas kernels for 0% -> 0%
where the time goes in v3:
time: 95.9 us; the launch traced here: 95.2 us
  Pallas kernels  94.5 us (99%)
    pallas_call x1, Pallas kernels, shards(): pl.pallas_call(functools.partial(kernel, factor), out_shape=(pltpu.VMEM((...  93.2 us

profile of v3, /device:TPU:8, one launch (start us, length us, event | category | flops | bytes accessed | tf_op | source)
XLA Modules:
  0.0 95.2 jit_solution(12260512727976944149)
XLA Ops:
  0.6 93.2 %shard_map.84 = (bf16[256,512]{1,0:T(8,128)(2,1)S(1)}, f32[1024,128]{1,0:T(8,128)S(1)}, f32[1024,128]{1,0:T(8,128)S(1)}, f32[128,1024]{1,0:T(8,128)S(1)}) custom-call(bf16[256,512]{1,0:T(8,128)(2,1)} %tok_ref.1, bf16[256,512]{1,0:T(8,128)(2,1)} %grd_ref.1, bf16[1024,128]{1,0:T(8,128)(2,1)} %gate_ref.1, bf16[1024,128]{1,0:T(8,128)(2,1)} %up_ref.1, ...), custom_call_target="tpu_custom_call" | custom-call | tf_op jit(solution)/shard_map/pallas_call | solution.py:548
  93.9 1.3 %shard_map.85 = (bf16[256,512]{1,0:T(8,128)(2,1)}, f32[1024,128]{1,0:T(8,128)}, f32[1024,128]{1,0:T(8,128)}, f32[128,1024]{1,0:T(8,128)}) custom-call(bf16[256,512]{1,0:T(8,128)(2,1)S(1)} %get-tuple-element.8.a, f32[1024,128]{1,0:T(8,128)S(1)} %get-tuple-element.9.b, f32[1024,128]{1,0:T(8,128)S(1)} %get-tuple-element.10.c, f32[128,1024]{1,0:T(8,128)S(1)} %get-tuple-element.11.d), custom_call_target="tpu_custom_call" | custom-call | tf_op jit(solution)/shard_map/pallas_call | solution.py:592

commit v4 on v3

--- a/solution.py
+++ b/solution.py
@@ -10,13 +10,14 @@
 
 MESH = pl.DeviceIdType.MESH
 F32, BF16 = jnp.float32, jnp.bfloat16
-COPIES = 200
+COPIES = 180
 
 
 class Copy:
-    def __init__(self, sems, src, dst, to, here=None):
-        index = sems[2][0]
-        sems[2][0] += 1
+    def __init__(self, sems, src, dst, to, here=None, index=None):
+        if index is None:
+            index = sems[2][0]
+            sems[2][0] += 1
         send, recv = sems[0].at[index], sems[1].at[index]
         self.remote = pltpu.make_async_remote_copy(
             src_ref=src, dst_ref=dst, send_sem=send, recv_sem=recv, device_id=to, device_id_type=MESH
@@ -61,7 +62,7 @@
     factor,
     tok_ref, grd_ref, gate_ref, up_ref, down_ref,
     ig_ref, gg_ref, ug_ref, dg_ref,
-    TV, WV, WDV, G, GT, WG, WD, PS, DR, RF, RN, GU, DL, X, XF, XN, IB,
+    TV, WV, WDV, G, GT, WG, WD, PS, DR, RF, RN, GU, DL, X, XF, XN, IB, BB,
     Z, ZS, ZF, ZN, S, SX, SD,
     send, recv, local_sem, load_sem,
 ):
@@ -77,8 +78,8 @@
     def dev(x=x, y=y, z=z, c=c):
         return (lax.div(z, 2) * 4 + y, (lax.rem(z, 2) * 4 + x) * 2 + c)
 
-    def copy(src, dst, to, here=None):
-        made = Copy(sems, src, dst, to, here)
+    def copy(src, dst, to, here=None, index=None):
+        made = Copy(sems, src, dst, to, here, index)
         sent.append(made)
         return made.start()
 
@@ -191,13 +192,15 @@
         gp[a, other] = copy(slot, slot, dev(x=xp))
         gm[a, other] = copy(slot, slot, dev(x=xm))
 
-    def pass_tokens(a):
-        gp[a, 0].wait()
-        slot = G.at[a, l, :, xm]
-        far_g[a, 0] = copy(slot, slot, dev(x=xp))
-        gm[a, 1].wait()
-        slot = G.at[a, ll, :, xp]
-        far_g[a, 1] = copy(slot, slot, dev(x=xm))
+    def pass_tokens(a, side):
+        if side == 0:
+            gp[a, 0].wait()
+            slot = G.at[a, l, :, xm]
+            far_g[a, 0] = copy(slot, slot, dev(x=xp))
+        else:
+            gm[a, 1].wait()
+            slot = G.at[a, ll, :, xp]
+            far_g[a, 1] = copy(slot, slot, dev(x=xm))
 
     def tokens_here(a):
         gp[a, 1].wait()
@@ -309,6 +312,8 @@
         dm[group, 1].wait()
         part = delta_at(group, yp, 1)
         far_d[group, 1] = copy(part, part, dev(y=ym))
+
+    def give_over(group):
         dp[group, 1].wait()
         over[group].append(copy(delta_at(group, ym), delta_at(group, ym), twin))
         dm[group, 0].wait()
@@ -417,95 +422,131 @@
             for half in range(2):
                 xnear[q, side, half].wait()
         for k in range(2):
-            IB[k, pl.ds(2 * q, 2)] = (X[q, x, k] + XN[q, 0, k] + XN[q, 1, k]).astype(BF16).reshape(2, 32, 512)
-
-    back = {}
+            IB[pl.ds(2 * q, 2), k] = (X[q, x, k] + XN[q, 0, k] + XN[q, 1, k]).astype(BF16).reshape(2, 32, 512)
+
+    FIRST, SECOND = COPIES, COPIES + 4
+
+    def arrives(index, ref):
+        return pltpu.make_async_copy(ref, ref, recv.at[index])
 
     def send_back(q):
-        for other in (1, 0):
-            for e in (2 * q, 2 * q + 1):
-                back[other, e] = copy(
-                    IB.at[ll if other else l, e],
+        for e in (2 * q, 2 * q + 1):
+            far = turn(y - x, e)
+            copy_back(IB.at[e], BB.at[far], dev(y=turn(x, -e)), far == 0, FIRST + far)
+
+    def copy_back(src, dst, to, here, index):
+        made = Copy(sems, src, dst, to, here, index)
+        made.done = True
+        sent.append(made.start())
+
+    def pass_back():
+        for d in range(4):
+            arrives(FIRST + d, BB.at[d]).wait()
+            to_x = turn(y, d)
+            far = turn(to_x - x, 0)
+            for other in (1, 0):
+                copy_back(
+                    BB.at[d, ll if other else l],
                     ig_ref.at[pl.ds(pl.multiple_of(l * 128 + x * 32, 32), 32), :],
-                    dev(x=y, y=turn(x, -e), z=zo if other else z),
-                    diagonal if e == 0 and not other else None,
+                    dev(x=to_x, z=zo if other else z),
+                    None if other else far == 0,
+                    SECOND + 2 * far + other,
                 )
+
+    def back_here():
+        for n in range(8):
+            arrives(SECOND + n, ig_ref.at[pl.ds(0, 32), :]).wait()
 
     GATE_UP, HIDDEN = 0, 1
     both = (0, 2)
     gate_up = [((part, part + 1), both, both) for part in range(2)]
     down = [(both, (2, 3), (q, q + 1)) for q in range(2)]
-    hidden = (both, (2, 3), both)
+    hidden = [((part, part + 1), (2, 3), both) for part in range(2)]
     deltas = [(both, both, (q, q + 1)) for q in range(2)]
     move(0)
-    for i in range(3):
+    for i in range(2):
         send_weights(i)
         for s in range(2):
             send_weights_to(i, s, False)
             send_weights_to(i, s, True)
         if i == 0:
             move(1)
+    send_weights(2)
+    send_weights_to(2, 0, True)
     spread(0, 0)
     spread(0, 1)
+    pass_weights(0, 0)
+    pass_tokens(0, 0)
+    pass_tokens(0, 1)
     spread(1, 0)
-    pass_weights(0, 0)
-    pass_tokens(0)
     spread(1, 1)
     pass_weights(0, 1)
     pass_weights(1, 1)
+    send_weights_to(2, 0, False)
     pass_weights(1, 0)
+    send_weights_to(2, 1, True)
+    send_weights_to(2, 1, False)
     tokens_here(0)
     weights_here(0, 0)
     weights_here(1, 0)
     multiply(gate_up[0])
-    pass_tokens(1)
     sum_start(gate_up[0])
+    pass_tokens(1, 0)
+    pass_tokens(1, 1)
     weights_here(0, 1)
     weights_here(1, 1)
     multiply(gate_up[1])
+    sum_middle(gate_up[0])
     pass_weights(2, 0)
+    sum_start(gate_up[1])
     pass_weights(2, 1)
-    sum_middle(gate_up[0])
-    sum_start(gate_up[1])
     for k in range(2):
         GT[k] = gathered(0, k).T
+    make_hidden(gate_up[0])
+    give(hidden[0])
+    sum_middle(gate_up[1])
     tokens_here(1)
     weights_here(2, 0)
     weights_here(2, 1)
     multiply(down[0])
     multiply(down[1])
-    sum_middle(gate_up[1])
-    make_hidden(gate_up[0])
+    give_on(hidden[0])
+    give_over(hidden[0])
     sum_start(down[0])
     sum_start(down[1])
     make_hidden(gate_up[1])
-    give(hidden)
+    give(hidden[1])
+    give_end(hidden[0])
     sum_middle(down[0])
     sum_middle(down[1])
-    give_on(hidden)
+    given(hidden[0])
+    grads_of_weights(2, 0)
+    wsum_near(2)
+    give_on(hidden[1])
+    give_over(hidden[1])
     make_deltas(down[0])
     give(deltas[0])
     make_deltas(down[1])
     give(deltas[1])
-    give_end(hidden)
-    given(hidden)
+    give_end(hidden[1])
+    given(hidden[1])
     grads_of_weights(2, 1)
     wsum_far(2)
-    grads_of_weights(2, 0)
-    wsum_near(2)
     give_on(deltas[0])
+    give_over(deltas[0])
     give_on(deltas[1])
+    give_over(deltas[1])
     give_end(deltas[0])
     give_end(deltas[1])
     given(deltas[0])
     input_rows(0)
     isum_start(0)
-    wsum_middle(2)
     given(deltas[1])
     grads_of_weights(0, 1)
     wsum_far(0)
     grads_of_weights(0, 0)
     wsum_near(0)
+    wsum_middle(2)
     input_rows(1)
     isum_start(1)
     grads_of_weights(1, 1)
@@ -515,18 +556,20 @@
     isum_middle(0)
     isum_middle(1)
     wsum_middle(0)
-    wsum_middle(1)
-    wsum_end(2)
     isum_end(0)
     send_back(0)
+    wsum_middle(1)
     isum_end(1)
     send_back(1)
+    wsum_end(2)
+    pass_back()
     wsum_end(0)
     wsum_end(1)
-    for made in [*last, *back.values()]:
+    back_here()
+    for made in last:
         made.wait()
     for made in sent:
-        assert made.done
+        assert made.done and sems[2][0] <= COPIES
         made.sent()
 
 
@@ -572,7 +615,8 @@
                 pltpu.VMEM((2, 4, 2, 64, 512), F32),
                 pltpu.VMEM((2, 2, 64, 512), F32),
                 pltpu.VMEM((2, 2, 2, 64, 512), F32),
-                pltpu.VMEM((2, 4, 32, 512), BF16),
+                pltpu.VMEM((4, 2, 32, 512), BF16),
+                pltpu.VMEM((4, 2, 32, 512), BF16),
                 pltpu.VMEM((3, 4, 2, 256, 256), F32),
                 pltpu.VMEM((3, 3, 2, 256, 256), BF16),
                 pltpu.VMEM((3, 2, 256, 256), BF16),
@@ -580,8 +624,8 @@
                 pltpu.VMEM((2, 512, 128), F32),
                 pltpu.VMEM((2, 512, 128), F32),
                 pltpu.VMEM((128, 512), F32),
-                pltpu.SemaphoreType.DMA((COPIES,)),
-                pltpu.SemaphoreType.DMA((COPIES,)),
+                pltpu.SemaphoreType.DMA((COPIES + 12,)),
+                pltpu.SemaphoreType.DMA((COPIES + 12,)),
                 pltpu.SemaphoreType.DMA((3,)),
                 pltpu.SemaphoreType.DMA((5,)),
             ],

time: 95.9 us -> 90.7 us (0.946)
  Pallas kernels: 94.5 us -> 90 us
    pallas_call x1, Pallas kernels: 93.2 us -> 88.7 us  [shards(): pl.pallas_call(functools.partial(kernel, factor), out_shape=(pltpu.VMEM((...]
where the time goes in v4:
time: 90.7 us; the launch traced here: 90.6 us
  Pallas kernels  90 us (99%)
    pallas_call x1, Pallas kernels, shards(): pl.pallas_call(functools.partial(kernel, factor), out_shape=(pltpu.VMEM((...  88.7 us

profile of v4, /device:TPU:8, one launch (start us, length us, event | category | flops | bytes accessed | tf_op | source)
XLA Modules:
  0.0 90.6 jit_solution(2916156769518813241)
XLA Ops:
  0.6 88.7 %shard_map.84 = (bf16[256,512]{1,0:T(8,128)(2,1)S(1)}, f32[1024,128]{1,0:T(8,128)S(1)}, f32[1024,128]{1,0:T(8,128)S(1)}, f32[128,1024]{1,0:T(8,128)S(1)}) custom-call(bf16[256,512]{1,0:T(8,128)(2,1)} %tok_ref.1, bf16[256,512]{1,0:T(8,128)(2,1)} %grd_ref.1, bf16[1024,128]{1,0:T(8,128)(2,1)} %gate_ref.1, bf16[1024,128]{1,0:T(8,128)(2,1)} %up_ref.1, ...), custom_call_target="tpu_custom_call" | custom-call | tf_op jit(solution)/shard_map/pallas_call | solution.py:591
  89.3 1.3 %shard_map.85 = (bf16[256,512]{1,0:T(8,128)(2,1)}, f32[1024,128]{1,0:T(8,128)}, f32[1024,128]{1,0:T(8,128)}, f32[128,1024]{1,0:T(8,128)}) custom-call(bf16[256,512]{1,0:T(8,128)(2,1)S(1)} %get-tuple-element.8.a, f32[1024,128]{1,0:T(8,128)S(1)} %get-tuple-element.9.b, f32[1024,128]{1,0:T(8,128)S(1)} %get-tuple-element.10.c, f32[128,1024]{1,0:T(8,128)S(1)} %get-tuple-element.11.d), custom_call_target="tpu_custom_call" | custom-call | tf_op jit(solution)/shard_map/pallas_call | solution.py:636

commit v5 on v4

--- a/solution.py
+++ b/solution.py
@@ -62,7 +62,7 @@
     factor,
     tok_ref, grd_ref, gate_ref, up_ref, down_ref,
     ig_ref, gg_ref, ug_ref, dg_ref,
-    TV, WV, WDV, G, GT, WG, WD, PS, DR, RF, RN, GU, DL, X, XF, XN, IB, BB,
+    TV, WV, WDV, G, GT, WG, WD, PS, DR, RF, RN, GU, DL, X, XB, XF, XN, IB, BB,
     Z, ZS, ZF, ZN, S, SX, SD,
     send, recv, local_sem, load_sem,
 ):
@@ -106,7 +106,7 @@
     barrier = pltpu.get_barrier_semaphore()
     peers = [
         twin, dev(x=xp), dev(x=xm), dev(y=yp), dev(y=ym),
-        dev(z=zp), dev(z=zm), dev(z=zp, c=cc), dev(z=zm, c=cc),
+        dev(z=zp), dev(z=zm), dev(z=zf), dev(z=zp, c=cc), dev(z=zm, c=cc),
     ]
     for e in range(4):
         there, back_there = dict(x=turn(y, e), y=x), dict(x=y, y=turn(x, -e))
@@ -350,6 +350,11 @@
     zfar, znear = {}, {}
 
     def wsum_near(i):
+        if i == 2:
+            for side, to_z in enumerate((zo, zn)):
+                ZS[2, side] = Z[2, side].astype(BF16)
+                znear[2, side] = copy(ZS.at[2, side], ZN.at[2, side], dev(z=to_z))
+            return
         ZS[i, 0, 1] = Z[i, 0, 1].astype(BF16)
         znear[i, 0, 1] = copy(ZS.at[i, 0, 1], ZN.at[i, 0, 1], dev(z=zo))
         ZS[i, 1, 0] = Z[i, 1, 0].astype(BF16)
@@ -357,6 +362,9 @@
 
     def wsum_far(i):
         ZS[i, 2] = Z[i, 3].astype(BF16)
+        if i == 2:
+            zfar[2] = copy(ZS.at[2, 2], ZF.at[2], dev(z=zf))
+            return
         zfar[i, 0] = copy(ZS.at[i, 2, 0], ZF.at[i, 0], dev(z=zn))
         zfar[i, 1] = copy(ZS.at[i, 2, 1], ZF.at[i, 1], dev(z=zo))
 
@@ -372,13 +380,16 @@
     half_at = pl.ds(pl.multiple_of(c * 512, 512), 512)
 
     def wsum_end(i):
-        for side in range(2):
-            for half in range(2):
-                znear[i, side, half].wait()
-        done = [
-            (Z[i, 2, half] + ZN[i, 0, half].astype(F32) + ZN[i, 1, half].astype(F32)) * factor
-            for half in range(2)
-        ]
+        sums = []
+        for half in range(2):
+            for side in range(2):
+                znear[(i, side) if i == 2 else (i, side, half)].wait()
+            total = Z[i, 2, half] + ZN[i, 0, half].astype(F32) + ZN[i, 1, half].astype(F32)
+            if i == 2:
+                zfar[2].wait()
+                total = total + ZF[2, half].astype(F32)
+            sums.append(total)
+        done = [total * factor for total in sums]
         if i < 2:
             out = (gg_ref, ug_ref)[i]
             for half in range(2):
@@ -404,17 +415,18 @@
     xfar, xnear = {}, {}
 
     def isum_start(q):
-        xfar[q, 0] = copy(X.at[q, xf, 0], XF.at[q, 0], dev(x=xp))
-        xfar[q, 1] = copy(X.at[q, xf, 1], XF.at[q, 1], dev(x=xm))
+        XB[q] = X[q, xf].astype(BF16)
+        xfar[q, 0] = copy(XB.at[q, 0], XF.at[q, 0], dev(x=xp))
+        xfar[q, 1] = copy(XB.at[q, 1], XF.at[q, 1], dev(x=xm))
         xnear[q, 0, 1] = copy(X.at[q, xp, 1], XN.at[q, 0, 1], dev(x=xp))
         xnear[q, 1, 0] = copy(X.at[q, xm, 0], XN.at[q, 1, 0], dev(x=xm))
 
     def isum_middle(q):
         xfar[q, 0].wait()
-        X[q, xp, 0] += XF[q, 0]
+        X[q, xp, 0] += XF[q, 0].astype(F32)
         xnear[q, 0, 0] = copy(X.at[q, xp, 0], XN.at[q, 0, 0], dev(x=xp))
         xfar[q, 1].wait()
-        X[q, xm, 1] += XF[q, 1]
+        X[q, xm, 1] += XF[q, 1].astype(F32)
         xnear[q, 1, 1] = copy(X.at[q, xm, 1], XN.at[q, 1, 1], dev(x=xm))
 
     def isum_end(q):
@@ -464,13 +476,17 @@
     hidden = [((part, part + 1), (2, 3), both) for part in range(2)]
     deltas = [(both, both, (q, q + 1)) for q in range(2)]
     move(0)
-    for i in range(2):
-        send_weights(i)
-        for s in range(2):
-            send_weights_to(i, s, False)
-            send_weights_to(i, s, True)
-        if i == 0:
-            move(1)
+    send_weights(0)
+    send_weights_to(0, 0, False)
+    send_weights_to(0, 0, True)
+    send_weights_to(0, 1, False)
+    send_weights_to(0, 1, True)
+    move(1)
+    send_weights(1)
+    send_weights_to(1, 0, False)
+    send_weights_to(1, 0, True)
+    send_weights_to(1, 1, False)
+    send_weights_to(1, 1, True)
     send_weights(2)
     send_weights_to(2, 0, True)
     spread(0, 0)
@@ -481,33 +497,33 @@
     spread(1, 0)
     spread(1, 1)
     pass_weights(0, 1)
+    weights_here(0, 0)
     pass_weights(1, 1)
     send_weights_to(2, 0, False)
     pass_weights(1, 0)
     send_weights_to(2, 1, True)
     send_weights_to(2, 1, False)
     tokens_here(0)
-    weights_here(0, 0)
     weights_here(1, 0)
     multiply(gate_up[0])
     sum_start(gate_up[0])
     pass_tokens(1, 0)
-    pass_tokens(1, 1)
     weights_here(0, 1)
     weights_here(1, 1)
     multiply(gate_up[1])
     sum_middle(gate_up[0])
     pass_weights(2, 0)
     sum_start(gate_up[1])
+    pass_tokens(1, 1)
     pass_weights(2, 1)
     for k in range(2):
         GT[k] = gathered(0, k).T
     make_hidden(gate_up[0])
     give(hidden[0])
     sum_middle(gate_up[1])
-    tokens_here(1)
     weights_here(2, 0)
     weights_here(2, 1)
+    tokens_here(1)
     multiply(down[0])
     multiply(down[1])
     give_on(hidden[0])
@@ -546,7 +562,6 @@
     wsum_far(0)
     grads_of_weights(0, 0)
     wsum_near(0)
-    wsum_middle(2)
     input_rows(1)
     isum_start(1)
     grads_of_weights(1, 1)
@@ -613,7 +628,8 @@
                 pltpu.VMEM((2, 2, 2, 2, 32, 128), F32),
                 pltpu.VMEM((2, 2, 4, 3, 2, 2, 32, 128), BF16),
                 pltpu.VMEM((2, 4, 2, 64, 512), F32),
-                pltpu.VMEM((2, 2, 64, 512), F32),
+                pltpu.VMEM((2, 2, 64, 512), BF16),
+                pltpu.VMEM((2, 2, 64, 512), BF16),
                 pltpu.VMEM((2, 2, 2, 64, 512), F32),
                 pltpu.VMEM((4, 2, 32, 512), BF16),
                 pltpu.VMEM((4, 2, 32, 512), BF16),

time: 90.7 us -> 87.6 us (0.966)
  Pallas kernels: 90 us -> 86.9 us
    pallas_call x1, Pallas kernels: 88.7 us -> 85.6 us  [shards(): pl.pallas_call(functools.partial(kernel, factor), out_shape=(pltpu.VMEM((...]
where the time goes in v5:
time: 87.6 us; the launch traced here: 87.5 us
  Pallas kernels  86.9 us (99%)
    pallas_call x1, Pallas kernels, shards(): pl.pallas_call(functools.partial(kernel, factor), out_shape=(pltpu.VMEM((...  85.6 us

profile of v5, /device:TPU:8, one launch (start us, length us, event | category | flops | bytes accessed | tf_op | source)
XLA Modules:
  0.0 87.5 jit_solution(15547677288176354233)
XLA Ops:
  0.6 85.6 %shard_map.84 = (bf16[256,512]{1,0:T(8,128)(2,1)S(1)}, f32[1024,128]{1,0:T(8,128)S(1)}, f32[1024,128]{1,0:T(8,128)S(1)}, f32[128,1024]{1,0:T(8,128)S(1)}) custom-call(bf16[256,512]{1,0:T(8,128)(2,1)} %tok_ref.1, bf16[256,512]{1,0:T(8,128)(2,1)} %grd_ref.1, bf16[1024,128]{1,0:T(8,128)(2,1)} %gate_ref.1, bf16[1024,128]{1,0:T(8,128)(2,1)} %up_ref.1, ...), custom_call_target="tpu_custom_call" | custom-call | tf_op jit(solution)/shard_map/pallas_call | solution.py:606
  86.2 1.3 %shard_map.85 = (bf16[256,512]{1,0:T(8,128)(2,1)}, f32[1024,128]{1,0:T(8,128)}, f32[1024,128]{1,0:T(8,128)}, f32[128,1024]{1,0:T(8,128)}) custom-call(bf16[256,512]{1,0:T(8,128)(2,1)S(1)} %get-tuple-element.8.a, f32[1024,128]{1,0:T(8,128)S(1)} %get-tuple-element.9.b, f32[1024,128]{1,0:T(8,128)S(1)} %get-tuple-element.10.c, f32[128,1024]{1,0:T(8,128)S(1)} %get-tuple-element.11.d), custom_call_target="tpu_custom_call" | custom-call | tf_op jit(solution)/shard_map/pallas_call | solution.py:652

commit v6 on v5

--- a/solution.py
+++ b/solution.py
@@ -10,7 +10,7 @@
 
 MESH = pl.DeviceIdType.MESH
 F32, BF16 = jnp.float32, jnp.bfloat16
-COPIES = 180
+COPIES = 200
 
 
 class Copy:
@@ -46,6 +46,23 @@
             pl.when(jnp.logical_not(self.here))(self.remote.wait_send)
 
 
+class View:
+    def __init__(self, ref, *lead):
+        self.ref, self.lead = ref, lead
+
+    def place(self, key):
+        return (*self.lead, *(key if isinstance(key, tuple) else (key,)))
+
+    def __getitem__(self, key):
+        return self.ref[self.place(key)]
+
+    def __setitem__(self, key, value):
+        self.ref[self.place(key)] = value
+
+    def at(self, *key):
+        return self.ref.at[self.place(key)]
+
+
 def nt(a, b):
     return lax.dot_general(a, b, (((1,), (1,)), ((), ())), preferred_element_type=F32)
 
@@ -63,7 +80,7 @@
     tok_ref, grd_ref, gate_ref, up_ref, down_ref,
     ig_ref, gg_ref, ug_ref, dg_ref,
     TV, WV, WDV, G, GT, WG, WD, PS, DR, RF, RN, GU, DL, X, XB, XF, XN, IB, BB,
-    Z, ZS, ZF, ZN, S, SX, SD,
+    Z, ZS, ZF, ZN, ZU, ZSU, ZFU, ZNU, S, SX, SD,
     send, recv, local_sem, load_sem,
 ):
     f, t = lax.axis_index("fsdp"), lax.axis_index("tp")
@@ -328,18 +345,22 @@
         for made in over[group]:
             made.wait()
 
-    def delta(kind, part, q):
-        return jnp.concatenate([DL[part, :, :, kind, q, half].reshape(256, 128) for half in range(2)], axis=1)
-
-    def delta_all(kind, part):
-        return jnp.concatenate([delta(kind, part, 0), delta(kind, part, 1)], axis=0)
+    def delta(kind, part, q, owners=(0, 1)):
+        return jnp.concatenate([DL[part, :, :, kind, q, half].reshape(256, 128) for half in owners], axis=1)
+
+    def delta_all(kind, part, owners=(0, 1)):
+        return jnp.concatenate([delta(kind, part, q, owners) for q in range(2)], axis=0)
 
     halves = (h, 1 - h)
 
     def grads_of_weights(i, part):
         for r in range(2):
-            if i < 2:
-                Z[i, 2 * part + r] = nn(GT[halves[r]], delta_all(i, part)).reshape(2, 256, 256)
+            if i == 0:
+                Z[0, 2 * part + r] = nn(GT[halves[r]], delta_all(0, part)).reshape(2, 256, 256)
+            elif i == 1:
+                block = nn(GT[halves[r]], delta_all(1, part, (cc, c))).reshape(2, 256, 256)
+                ZU[0, 2 * part + r] = block[:, :, :128]
+                ZU[1, 2 * part + r] = block[:, :, 128:]
             else:
                 block = tn(delta_all(2, part), gathered(1, halves[r]))
                 for j in range(2):
@@ -349,55 +370,70 @@
 
     zfar, znear = {}, {}
 
+    def stream(i):
+        if i in (0, 2):
+            return [View(ref, i) for ref in (Z, ZS, ZF, ZN)]
+        return [View(ref, i // 2) for ref in (ZU, ZSU, ZFU, ZNU)]
+
     def wsum_near(i):
+        part, out, _, near = stream(i)
         if i == 2:
             for side, to_z in enumerate((zo, zn)):
-                ZS[2, side] = Z[2, side].astype(BF16)
-                znear[2, side] = copy(ZS.at[2, side], ZN.at[2, side], dev(z=to_z))
+                out[side] = part[side].astype(BF16)
+                znear[2, side] = copy(out.at(side), near.at(side), dev(z=to_z))
             return
-        ZS[i, 0, 1] = Z[i, 0, 1].astype(BF16)
-        znear[i, 0, 1] = copy(ZS.at[i, 0, 1], ZN.at[i, 0, 1], dev(z=zo))
-        ZS[i, 1, 0] = Z[i, 1, 0].astype(BF16)
-        znear[i, 1, 0] = copy(ZS.at[i, 1, 0], ZN.at[i, 1, 0], dev(z=zn))
+        out[0, 1] = part[0, 1].astype(BF16)
+        znear[i, 0, 1] = copy(out.at(0, 1), near.at(0, 1), dev(z=zo))
+        out[1, 0] = part[1, 0].astype(BF16)
+        znear[i, 1, 0] = copy(out.at(1, 0), near.at(1, 0), dev(z=zn))
 
     def wsum_far(i):
-        ZS[i, 2] = Z[i, 3].astype(BF16)
+        part, out, far, _ = stream(i)
+        out[2] = part[3].astype(BF16)
         if i == 2:
-            zfar[2] = copy(ZS.at[2, 2], ZF.at[2], dev(z=zf))
+            zfar[2] = copy(out.at(2), far.at(), dev(z=zf))
             return
-        zfar[i, 0] = copy(ZS.at[i, 2, 0], ZF.at[i, 0], dev(z=zn))
-        zfar[i, 1] = copy(ZS.at[i, 2, 1], ZF.at[i, 1], dev(z=zo))
+        zfar[i, 0] = copy(out.at(2, 0), far.at(0), dev(z=zn))
+        zfar[i, 1] = copy(out.at(2, 1), far.at(1), dev(z=zo))
 
     def wsum_middle(i):
+        part, out, far, near = stream(i)
         zfar[i, 0].wait()
-        ZS[i, 0, 0] = (Z[i, 0, 0] + ZF[i, 0].astype(F32)).astype(BF16)
-        znear[i, 0, 0] = copy(ZS.at[i, 0, 0], ZN.at[i, 0, 0], dev(z=zo))
+        out[0, 0] = (part[0, 0] + far[0].astype(F32)).astype(BF16)
+        znear[i, 0, 0] = copy(out.at(0, 0), near.at(0, 0), dev(z=zo))
         zfar[i, 1].wait()
-        ZS[i, 1, 1] = (Z[i, 1, 1] + ZF[i, 1].astype(F32)).astype(BF16)
-        znear[i, 1, 1] = copy(ZS.at[i, 1, 1], ZN.at[i, 1, 1], dev(z=zn))
+        out[1, 1] = (part[1, 1] + far[1].astype(F32)).astype(BF16)
+        znear[i, 1, 1] = copy(out.at(1, 1), near.at(1, 1), dev(z=zn))
 
     last = []
     half_at = pl.ds(pl.multiple_of(c * 512, 512), 512)
 
     def wsum_end(i):
+        part, _, far, near = stream(i)
         sums = []
         for half in range(2):
             for side in range(2):
                 znear[(i, side) if i == 2 else (i, side, half)].wait()
-            total = Z[i, 2, half] + ZN[i, 0, half].astype(F32) + ZN[i, 1, half].astype(F32)
+            total = part[2, half] + near[0, half].astype(F32) + near[1, half].astype(F32)
             if i == 2:
                 zfar[2].wait()
-                total = total + ZF[2, half].astype(F32)
+                total = total + far[half].astype(F32)
             sums.append(total)
         done = [total * factor for total in sums]
-        if i < 2:
-            out = (gg_ref, ug_ref)[i]
+        if i == 0:
             for half in range(2):
                 low, high = done[half][:, :128], done[half][:, 128:]
-                SX[i, pl.ds(half * 256, 256), :] = jnp.where(c == 0, high, low)
-                S[i, pl.ds(half * 256, 256), :] = jnp.where(c == 0, low, high)
-            last.append(copy(SX.at[i], out.at[half_at, :], twin))
-            out[half_at, :] = S[i]
+                SX[0, pl.ds(half * 256, 256), :] = jnp.where(c == 0, high, low)
+                S[0, pl.ds(half * 256, 256), :] = jnp.where(c == 0, low, high)
+            last.append(copy(SX.at[0], gg_ref.at[half_at, :], twin))
+            gg_ref[half_at, :] = S[0]
+        elif i == 1:
+            for half in range(2):
+                SX[1, pl.ds(half * 256, 256), :] = done[half]
+            last.append(copy(SX.at[1], ug_ref.at[half_at, :], twin))
+        elif i == 3:
+            for half in range(2):
+                ug_ref[pl.ds(pl.multiple_of(c * 512 + half * 256, 256), 256), :] = done[half]
         else:
             blocks = [jnp.concatenate([part[:128], part[128:]], axis=1) for part in done]
             SD[...] = jnp.where(c == 0, blocks[1], blocks[0])
@@ -410,7 +446,9 @@
             right = jnp.concatenate(
                 [WG[kind, k, 2 * sides[part] + b] for part in range(2) for kind in range(2) for b in range(2)], axis=1
             )
-            X[q, :, k] = nt(left, right).reshape(4, 64, 512)
+            term = nt(left, right).reshape(4, 2, 32, 512)
+            X[2 * q, :, k] = term[:, 0]
+            X[2 * q + 1, :, k] = term[:, 1]
 
     xfar, xnear = {}, {}
 
@@ -434,17 +472,16 @@
             for half in range(2):
                 xnear[q, side, half].wait()
         for k in range(2):
-            IB[pl.ds(2 * q, 2), k] = (X[q, x, k] + XN[q, 0, k] + XN[q, 1, k]).astype(BF16).reshape(2, 32, 512)
+            IB[q, k] = (X[q, x, k] + XN[q, 0, k] + XN[q, 1, k]).astype(BF16)
 
     FIRST, SECOND = COPIES, COPIES + 4
 
     def arrives(index, ref):
         return pltpu.make_async_copy(ref, ref, recv.at[index])
 
-    def send_back(q):
-        for e in (2 * q, 2 * q + 1):
-            far = turn(y - x, e)
-            copy_back(IB.at[e], BB.at[far], dev(y=turn(x, -e)), far == 0, FIRST + far)
+    def send_back(e):
+        far = turn(y - x, e)
+        copy_back(IB.at[e], BB.at[far], dev(y=turn(x, -e)), far == 0, FIRST + far)
 
     def copy_back(src, dst, to, here, index):
         made = Copy(sems, src, dst, to, here, index)
@@ -488,19 +525,19 @@
     send_weights_to(1, 1, False)
     send_weights_to(1, 1, True)
     send_weights(2)
-    send_weights_to(2, 0, True)
     spread(0, 0)
     spread(0, 1)
     pass_weights(0, 0)
     pass_tokens(0, 0)
     pass_tokens(0, 1)
+    pass_weights(0, 1)
     spread(1, 0)
     spread(1, 1)
-    pass_weights(0, 1)
     weights_here(0, 0)
     pass_weights(1, 1)
     send_weights_to(2, 0, False)
     pass_weights(1, 0)
+    send_weights_to(2, 0, True)
     send_weights_to(2, 1, True)
     send_weights_to(2, 1, False)
     tokens_here(0)
@@ -557,29 +594,41 @@
     given(deltas[0])
     input_rows(0)
     isum_start(0)
+    isum_start(1)
     given(deltas[1])
     grads_of_weights(0, 1)
     wsum_far(0)
     grads_of_weights(0, 0)
     wsum_near(0)
     input_rows(1)
-    isum_start(1)
+    isum_start(2)
+    isum_start(3)
     grads_of_weights(1, 1)
     wsum_far(1)
+    wsum_far(3)
     grads_of_weights(1, 0)
     wsum_near(1)
+    wsum_near(3)
     isum_middle(0)
     isum_middle(1)
+    isum_middle(2)
+    isum_middle(3)
     wsum_middle(0)
     isum_end(0)
     send_back(0)
     wsum_middle(1)
+    wsum_middle(3)
     isum_end(1)
     send_back(1)
+    isum_end(2)
+    send_back(2)
+    isum_end(3)
+    send_back(3)
     wsum_end(2)
     pass_back()
     wsum_end(0)
     wsum_end(1)
+    wsum_end(3)
     back_here()
     for made in last:
         made.wait()
@@ -627,16 +676,20 @@
                 pltpu.VMEM((2, 3, 2, 2, 2, 32, 128), F32),
                 pltpu.VMEM((2, 2, 2, 2, 32, 128), F32),
                 pltpu.VMEM((2, 2, 4, 3, 2, 2, 32, 128), BF16),
-                pltpu.VMEM((2, 4, 2, 64, 512), F32),
-                pltpu.VMEM((2, 2, 64, 512), BF16),
-                pltpu.VMEM((2, 2, 64, 512), BF16),
-                pltpu.VMEM((2, 2, 2, 64, 512), F32),
+                pltpu.VMEM((4, 4, 2, 32, 512), F32),
+                pltpu.VMEM((4, 2, 32, 512), BF16),
+                pltpu.VMEM((4, 2, 32, 512), BF16),
+                pltpu.VMEM((4, 2, 2, 32, 512), F32),
                 pltpu.VMEM((4, 2, 32, 512), BF16),
                 pltpu.VMEM((4, 2, 32, 512), BF16),
                 pltpu.VMEM((3, 4, 2, 256, 256), F32),
                 pltpu.VMEM((3, 3, 2, 256, 256), BF16),
                 pltpu.VMEM((3, 2, 256, 256), BF16),
                 pltpu.VMEM((3, 2, 2, 256, 256), BF16),
+                pltpu.VMEM((2, 4, 2, 256, 128), F32),
+                pltpu.VMEM((2, 3, 2, 256, 128), BF16),
+                pltpu.VMEM((2, 2, 256, 128), BF16),
+                pltpu.VMEM((2, 2, 2, 256, 128), BF16),
                 pltpu.VMEM((2, 512, 128), F32),
                 pltpu.VMEM((2, 512, 128), F32),
                 pltpu.VMEM((128, 512), F32),

time: 87.6 us -> 87 us (level)
  Pallas kernels: 86.9 us -> 86 us
where the time goes in v6:
time: 87 us; the launch traced here: 86.7 us
  Pallas kernels  86 us (99%)
    pallas_call x1, Pallas kernels, shards(): pl.pallas_call(functools.partial(kernel, factor), out_shape=(pltpu.VMEM((...  84.8 us

profile of v6, /device:TPU:8, one launch (start us, length us, event | category | flops | bytes accessed | tf_op | source)
XLA Modules:
  0.0 86.7 jit_solution(9529223570923874377)
XLA Ops:
  0.6 84.8 %shard_map.84 = (bf16[256,512]{1,0:T(8,128)(2,1)S(1)}, f32[1024,128]{1,0:T(8,128)S(1)}, f32[1024,128]{1,0:T(8,128)S(1)}, f32[128,1024]{1,0:T(8,128)S(1)}) custom-call(bf16[256,512]{1,0:T(8,128)(2,1)} %tok_ref.1, bf16[256,512]{1,0:T(8,128)(2,1)} %grd_ref.1, bf16[1024,128]{1,0:T(8,128)(2,1)} %gate_ref.1, bf16[1024,128]{1,0:T(8,128)(2,1)} %up_ref.1, ...), custom_call_target="tpu_custom_call" | custom-call | tf_op jit(solution)/shard_map/pallas_call | solution.py:655
  85.4 1.3 %shard_map.85 = (bf16[256,512]{1,0:T(8,128)(2,1)}, f32[1024,128]{1,0:T(8,128)}, f32[1024,128]{1,0:T(8,128)}, f32[128,1024]{1,0:T(8,128)}) custom-call(bf16[256,512]{1,0:T(8,128)(2,1)S(1)} %get-tuple-element.8.a, f32[1024,128]{1,0:T(8,128)S(1)} %get-tuple-element.9.b, f32[1024,128]{1,0:T(8,128)S(1)} %get-tuple-element.10.c, f32[128,1024]{1,0:T(8,128)S(1)} %get-tuple-element.11.d), custom_call_target="tpu_custom_call" | custom-call | tf_op jit(solution)/shard_map/pallas_call | solution.py:705

commit v7 on v6

--- a/solution.py
+++ b/solution.py
@@ -232,9 +232,10 @@
 
     def multiply(unit):
         parts, arrays_of, chunks = unit
-        for part in range(*parts):
-            l_to = sides[part]
-            for i in range(*arrays_of):
+        to_twin[unit] = []
+        for i in range(*arrays_of):
+            for part in range(*parts):
+                l_to = sides[part]
                 a = min(i // 2, 1)
                 total = None
                 for k in range(2):
@@ -251,7 +252,8 @@
                     PS[part, i, chunks[0] : chunks[1], :, :, half] = block.reshape(
                         chunks[1] - chunks[0], 2, 4, 32, 128
                     )
-        to_twin[unit] = copy(at(PS, unit, cc), at(DR, unit), twin)
+            one = (parts, (i, i + 1), chunks)
+            to_twin[unit].append(copy(at(PS, one, cc), at(DR, one), twin))
 
     to_twin, yfar, ynear = {}, {}, {}
 
@@ -263,7 +265,8 @@
         return [(p, i, q) for p in range(*parts) for i in range(*arrays_of) for q in range(*chunks)]
 
     def sum_start(unit):
-        to_twin[unit].wait()
+        for made in to_twin[unit]:
+            made.wait()
         for u in over_unit(unit):
             PS[(*u, c)] += DR[u]
         yfar[unit, 0] = copy(at(PS, unit, c, yf, 0), at(RF, unit, 0), dev(y=yp))

time: 87 us -> 86.8 us (level)
  no operation moved by 1% of the time
where the time goes in v7:
time: 86.8 us; the launch traced here: 86.6 us
  Pallas kernels  86 us (99%)
    pallas_call x1, Pallas kernels, shards(): pl.pallas_call(functools.partial(kernel, factor), out_shape=(pltpu.VMEM((...  84.7 us

profile of v7, /device:TPU:8, one launch (start us, length us, event | category | flops | bytes accessed | tf_op | source)
XLA Modules:
  0.0 86.6 jit_solution(11307965656724447677)
XLA Ops:
  0.6 84.7 %shard_map.84 = (bf16[256,512]{1,0:T(8,128)(2,1)S(1)}, f32[1024,128]{1,0:T(8,128)S(1)}, f32[1024,128]{1,0:T(8,128)S(1)}, f32[128,1024]{1,0:T(8,128)S(1)}) custom-call(bf16[256,512]{1,0:T(8,128)(2,1)} %tok_ref.1, bf16[256,512]{1,0:T(8,128)(2,1)} %grd_ref.1, bf16[1024,128]{1,0:T(8,128)(2,1)} %gate_ref.1, bf16[1024,128]{1,0:T(8,128)(2,1)} %up_ref.1, ...), custom_call_target="tpu_custom_call" | custom-call | tf_op jit(solution)/shard_map/pallas_call | solution.py:658
  85.4 1.3 %shard_map.85 = (bf16[256,512]{1,0:T(8,128)(2,1)}, f32[1024,128]{1,0:T(8,128)}, f32[1024,128]{1,0:T(8,128)}, f32[128,1024]{1,0:T(8,128)}) custom-call(bf16[256,512]{1,0:T(8,128)(2,1)S(1)} %get-tuple-element.8.a, f32[1024,128]{1,0:T(8,128)S(1)} %get-tuple-element.9.b, f32[1024,128]{1,0:T(8,128)S(1)} %get-tuple-element.10.c, f32[128,1024]{1,0:T(8,128)S(1)} %get-tuple-element.11.d), custom_call_target="tpu_custom_call" | custom-call | tf_op jit(solution)/shard_map/pallas_call | solution.py:708

commit v8 on v7

--- a/solution.py
+++ b/solution.py
@@ -546,6 +546,8 @@
     tokens_here(0)
     weights_here(1, 0)
     multiply(gate_up[0])
+    for k in range(2):
+        GT[k] = gathered(0, k).T
     sum_start(gate_up[0])
     pass_tokens(1, 0)
     weights_here(0, 1)
@@ -556,8 +558,6 @@
     sum_start(gate_up[1])
     pass_tokens(1, 1)
     pass_weights(2, 1)
-    for k in range(2):
-        GT[k] = gathered(0, k).T
     make_hidden(gate_up[0])
     give(hidden[0])
     sum_middle(gate_up[1])

time: 86.8 us -> 86.9 us (level)
  no operation moved by 1% of the time
where the time goes in v8:
time: 86.9 us; the launch traced here: 86.6 us
  Pallas kernels  86 us (99%)
    pallas_call x1, Pallas kernels, shards(): pl.pallas_call(functools.partial(kernel, factor), out_shape=(pltpu.VMEM((...  84.7 us

profile of v8, /device:TPU:8, one launch (start us, length us, event | category | flops | bytes accessed | tf_op | source)
XLA Modules:
  0.0 86.6 jit_solution(7764136998005280473)
XLA Ops:
  0.6 84.7 %shard_map.84 = (bf16[256,512]{1,0:T(8,128)(2,1)S(1)}, f32[1024,128]{1,0:T(8,128)S(1)}, f32[1024,128]{1,0:T(8,128)S(1)}, f32[128,1024]{1,0:T(8,128)S(1)}) custom-call(bf16[256,512]{1,0:T(8,128)(2,1)} %tok_ref.1, bf16[256,512]{1,0:T(8,128)(2,1)} %grd_ref.1, bf16[1024,128]{1,0:T(8,128)(2,1)} %gate_ref.1, bf16[1024,128]{1,0:T(8,128)(2,1)} %up_ref.1, ...), custom_call_target="tpu_custom_call" | custom-call | tf_op jit(solution)/shard_map/pallas_call | solution.py:658
  85.4 1.3 %shard_map.85 = (bf16[256,512]{1,0:T(8,128)(2,1)}, f32[1024,128]{1,0:T(8,128)}, f32[1024,128]{1,0:T(8,128)}, f32[128,1024]{1,0:T(8,128)}) custom-call(bf16[256,512]{1,0:T(8,128)(2,1)S(1)} %get-tuple-element.8.a, f32[1024,128]{1,0:T(8,128)S(1)} %get-tuple-element.9.b, f32[1024,128]{1,0:T(8,128)S(1)} %get-tuple-element.10.c, f32[128,1024]{1,0:T(8,128)S(1)} %get-tuple-element.11.d), custom_call_target="tpu_custom_call" | custom-call | tf_op jit(solution)/shard_map/pallas_call | solution.py:708
